TPU v7x, 256 devices: a whole 4x4x8 slice. The times are simulated.
256 devices in a mesh: group: 8 (over x, core), dev: 32 (over z, y).
Axes of the slice: x: 4, y: 4, z: 8, core: 2. Of those that a mesh axis runs over, the one named last changes fastest.
Arguments:
- state: float32 [5, 4, 4, 4, 16, 64, 128], P(None, None, None, None, 'group', 'dev'), may hold values from -3 to 19.25, as said below
- limit_slot: int32 [16, 64, 128], P('group', 'dev'), may hold values from -1 to 511, as said below
- wall_owner: int32 [16, 64, 2], P('group', 'dev'), may hold values from 0 to 2047
Outputs:
- state_next: float32 [5, 4, 4, 4, 16, 64, 128], P(None, None, None, None, 'group', 'dev')
- wall_loads: float32 [2048], P(('group', 'dev'))
Inputs may be any that keep to these rules, and one draw needn't show every extreme that they name: `state`: density lies in 0.5 to 2, each velocity component in -1.5 to 1.5 and p in 0.2 to 5 at every node. A troubled element has limit_slot = destination * 16 + slot, the destination an index of dev within the element's group and the slot below 16. The troubled elements of one device have distinct values and fill whole blocks of 16 slots per destination; one device has at most 512 troubled elements, some device of every group has exactly 512, and every device is the destination of exactly 128 troubled elements of its group.
All inputs are finite; a program needn't handle non-finite values.
Results may differ from a plain program's by a relative error of at most 0.00013.
Values sent between devices are 32-bit elements; how exact they have to be, the bound alone decides.
No kernel may reach another device: no remote copies, remote signals or barrier semaphores. Data moves between devices by JAX's collectives and lax.ppermute only.
A program may use at most 64 MiB of HBM per device.

v0:
```python
import jax
import jax.numpy as jnp
import numpy as np
from jax import lax
from jax.sharding import PartitionSpec as P

SUBSTEPS = 8
CAP = 16
SN_DEV = 8


gamma_ratio = 1.4
courant = 0.02


def with_halo(x, sides, width):
    for axis, dim in sides:
        devices, length = (lax.axis_size(axis), x.shape[dim])
        up = [(i, (i + 1) % devices) for i in range(devices)]
        down = [(j, i) for i, j in up]
        last = lax.slice_in_dim(x, length - width, length, axis=dim)
        first = lax.slice_in_dim(x, 0, width, axis=dim)
        before = lax.ppermute(last, axis, up)
        after = lax.ppermute(first, axis, down)
        x = jnp.concatenate([before, x, after], axis=dim)
    return x


def gll_tables():
    gll_nodes = np.array([-1.0, -np.sqrt(0.2), np.sqrt(0.2), 1.0])
    weights = np.array([1.0, 5.0, 5.0, 1.0]) / 6.0
    bary_weights = np.array(
        [
            1.0
            / np.prod(
                [
                    gll_nodes[index_a] - gll_nodes[index_b]
                    for index_b in range(4)
                    if index_b != index_a
                ]
            )
            for index_a in range(4)
        ]
    )
    derivative = np.zeros((4, 4))
    for index_a in range(4):
        for index_b in range(4):
            if index_a != index_b:
                derivative[index_a, index_b] = (
                    bary_weights[index_b]
                    / bary_weights[index_a]
                    / (gll_nodes[index_a] - gll_nodes[index_b])
                )
        derivative[index_a, index_a] = -np.sum(derivative[index_a])
    return (jnp.asarray(derivative, jnp.float32), jnp.asarray(weights, jnp.float32))


def euler_flux(conserved, direction):
    density = conserved[0]
    normal_velocity = conserved[1 + direction] / density
    pressure = (gamma_ratio - 1.0) * (
        conserved[4]
        - 0.5
        * (conserved[1] * conserved[1] + conserved[2] * conserved[2] + conserved[3] * conserved[3])
        / density
    )
    flux_rows = [conserved[1 + direction]]
    for component in range(3):
        momentum_flux = conserved[1 + component] * normal_velocity
        if component == direction:
            momentum_flux = momentum_flux + pressure
        flux_rows.append(momentum_flux)
    flux_rows.append(normal_velocity * (conserved[4] + pressure))
    wave_speed = jnp.abs(normal_velocity) + jnp.sqrt(gamma_ratio * pressure / density)
    return (jnp.stack(flux_rows), wave_speed)


def rusanov(left_state, right_state, direction):
    left_flux, left_speed = euler_flux(left_state, direction)
    right_flux, right_speed = euler_flux(right_state, direction)
    fastest = jnp.maximum(left_speed, right_speed)
    return 0.5 * (left_flux + right_flux) - 0.5 * fastest * (right_state - left_state)


def mirrored(conserved):
    return jnp.concatenate([conserved[:3], -conserved[3:4], conserved[4:]], axis=0)


def node_index(node_axis, which):
    return (slice(None),) * node_axis + (which,)


def dg_rate(state, direction, flux_low, flux_high, derivative, weights):
    node_flux, wave_speed = euler_flux(state, direction)
    einsum_forms = ["ai,vijk...->vajk...", "aj,vijk...->viak...", "ak,vijk...->vija..."]
    volume = jnp.einsum(
        einsum_forms[direction], derivative, node_flux, precision=lax.Precision.HIGHEST
    )
    node_axis = 1 + direction
    low_index = node_index(node_axis, 0)
    high_index = node_index(node_axis, 3)
    volume = volume.at[low_index].add(-(flux_low - node_flux[low_index]) / weights[0])
    volume = volume.at[high_index].add((flux_high - node_flux[high_index]) / weights[3])
    return volume


def fv_rate(state, direction, flux_low, flux_high, weights):
    node_axis = 1 + direction
    lower_nodes = lax.slice_in_dim(state, 0, 3, axis=node_axis)
    upper_nodes = lax.slice_in_dim(state, 1, 4, axis=node_axis)
    inner_flux = rusanov(lower_nodes, upper_nodes, direction)
    interfaces = jnp.concatenate(
        [jnp.expand_dims(flux_low, node_axis), inner_flux, jnp.expand_dims(flux_high, node_axis)],
        axis=node_axis,
    )
    width_shape = [1] * state.ndim
    width_shape[node_axis] = 4
    widths = weights.reshape(width_shape)
    upper_faces = lax.slice_in_dim(interfaces, 1, 5, axis=node_axis)
    lower_faces = lax.slice_in_dim(interfaces, 0, 4, axis=node_axis)
    return (upper_faces - lower_faces) / widths


def dg_next(state, fluxes, derivative, weights):
    rate_sum = dg_rate(state, 0, fluxes[0], fluxes[1], derivative, weights)
    rate_sum = rate_sum + dg_rate(state, 1, fluxes[2], fluxes[3], derivative, weights)
    rate_sum = rate_sum + dg_rate(state, 2, fluxes[4], fluxes[5], derivative, weights)
    return state - courant * rate_sum


def fv_next(state, fluxes, weights):
    sub_state = state
    for substep in range(SUBSTEPS):
        rate_sum = fv_rate(sub_state, 0, fluxes[0], fluxes[1], weights)
        rate_sum = rate_sum + fv_rate(sub_state, 1, fluxes[2], fluxes[3], weights)
        rate_sum = rate_sum + fv_rate(sub_state, 2, fluxes[4], fluxes[5], weights)
        sub_state = sub_state - courant / SUBSTEPS * rate_sum
    return sub_state


def z_fluxes(state):
    z_low, z_high = (state[:, :, :, 0], state[:, :, :, 3])
    below_states = jnp.concatenate([mirrored(z_low[..., 0:1]), z_high[..., :-1]], axis=-1)
    z_flux_low = rusanov(below_states, z_low, 2)
    top_flux = rusanov(z_high[..., -1:], mirrored(z_high[..., -1:]), 2)
    z_flux_high = jnp.concatenate([z_flux_low[..., 1:], top_flux], axis=-1)
    return (z_flux_low, z_flux_high, top_flux)


def wall_face_loads(z_flux_low, top_flux, weights):
    face_weights = weights[:, None] * weights[None, :]
    bottom_load = -jnp.sum(
        face_weights[:, :, None, None] * z_flux_low[3, :, :, :, :, 0], axis=(0, 1)
    )
    top_load = jnp.sum(face_weights[:, :, None, None] * top_flux[3, :, :, :, :, 0], axis=(0, 1))
    return jnp.stack([bottom_load, top_load], axis=-1)


def limit_columns(state_cols, flux_cols, positions, capacity, weights):
    packed_state = (
        jnp.ones((320, capacity), jnp.float32).at[:, positions].set(state_cols, mode="drop")
    )
    packed_flux = (
        jnp.ones((480, capacity), jnp.float32).at[:, positions].set(flux_cols, mode="drop")
    )
    face_list = [
        packed_flux[80 * face : 80 * (face + 1)].reshape(5, 4, 4, capacity) for face in range(6)
    ]
    limited_state = fv_next(packed_state.reshape(5, 4, 4, 4, capacity), face_list, weights)
    return limited_state.reshape(320, capacity)


def on_device(state, limit_slot, wall_owner):
    derivative, weights = gll_tables()
    n_dev = lax.axis_size("dev")
    x_low, x_high = (state[:, 0], state[:, 3])
    x_rim = jnp.stack([x_low[:, :, :, 0], x_high[:, :, :, -1]], axis=3)
    x_around = with_halo(x_rim, (("group", 3),), 1)
    x_flux = rusanov(
        jnp.concatenate([x_around[:, :, :, 0:1], x_high], axis=3),
        jnp.concatenate([x_low, x_around[:, :, :, 3:4]], axis=3),
        0,
    )
    y_low, y_high = (state[:, :, 0], state[:, :, 3])
    y_rim = jnp.stack([y_low[:, :, :, :, 0], y_high[:, :, :, :, -1]], axis=4)
    y_around = with_halo(y_rim, (("dev", 4),), 1)
    y_flux = rusanov(
        jnp.concatenate([y_around[:, :, :, :, 0:1], y_high], axis=4),
        jnp.concatenate([y_low, y_around[:, :, :, :, 3:4]], axis=4),
        1,
    )
    z_flux_low, z_flux_high, top_flux = z_fluxes(state)
    fluxes = [
        x_flux[:, :, :, :-1],
        x_flux[:, :, :, 1:],
        y_flux[:, :, :, :, :-1],
        y_flux[:, :, :, :, 1:],
        z_flux_low,
        z_flux_high,
    ]
    face_load = wall_face_loads(z_flux_low, top_flux, weights)
    load_flat = face_load.reshape(-1)
    owner_flat = wall_owner.reshape(-1)
    all_nodes = SN_DEV * lax.axis_size("group") * n_dev
    matches = owner_flat[:, None] == jnp.arange(all_nodes, dtype=jnp.int32)[None, :]
    partial_value = jnp.sum(jnp.where(matches, load_flat[:, None], 0.0), axis=0)
    wall_loads = lax.psum_scatter(partial_value, ("group", "dev"), scatter_dimension=0, tiled=True)
    dg_state = dg_next(state, fluxes, derivative, weights)
    elements = limit_slot.size
    state_cols = state.reshape(320, elements)
    flux_cols = jnp.stack([face.reshape(80, elements) for face in fluxes]).reshape(480, elements)
    slot_flat = limit_slot.reshape(elements)
    troubled = slot_flat >= 0
    slot_count = n_dev * CAP
    positions = jnp.where(troubled, slot_flat, slot_count)
    send_state = (
        jnp.zeros((320, slot_count), jnp.float32).at[:, positions].set(state_cols, mode="drop")
    )
    send_flux = (
        jnp.zeros((480, slot_count), jnp.float32).at[:, positions].set(flux_cols, mode="drop")
    )
    send_mark = jnp.zeros((1, slot_count), jnp.float32).at[0, positions].set(1.0, mode="drop")
    got_state, got_flux, got_mark = (
        lax.all_to_all(send_state, "dev", split_axis=1, concat_axis=1, tiled=True),
        lax.all_to_all(send_flux, "dev", split_axis=1, concat_axis=1, tiled=True),
        lax.all_to_all(send_mark, "dev", split_axis=1, concat_axis=1, tiled=True),
    )
    recv_count = 2 * (n_dev // 8) * CAP
    live_slots = got_mark[0] > 0.5
    live_rank = jnp.cumsum(live_slots.astype(jnp.int32)) - 1
    packed_at = jnp.where(live_slots, live_rank, recv_count)
    results = limit_columns(got_state, got_flux, packed_at, recv_count, weights)
    answers = jnp.where(
        live_slots[None, :], jnp.take(results, jnp.clip(packed_at, 0, recv_count - 1), axis=1), 0.0
    )
    returned = lax.all_to_all(answers, "dev", split_axis=1, concat_axis=1, tiled=True)
    limited = jnp.take(returned, jnp.clip(positions, 0, slot_count - 1), axis=1)
    state_next = jnp.where(troubled[None, :], limited, dg_state.reshape(320, elements)).reshape(
        state.shape
    )
    return (state_next, wall_loads)


def solution(mesh):
    in_specs = (
        P(None, None, None, None, "group", "dev", None),
        P("group", "dev", None),
        P("group", "dev", None),
    )
    out_specs = (P(None, None, None, None, "group", "dev", None), P(("group", "dev")))
    return jax.shard_map(
        on_device, mesh=mesh, in_specs=in_specs, out_specs=out_specs, check_vma=False
    )
```

profile of v0, /device:TPU:8, one launch (start us, length us, event | category | flops | bytes accessed | tf_op | source)
XLA Modules:
  0.0 411.7 jit_solution(12665995347298279065)
XLA Ops:
  0.6 1.3 compare_select_fusion.1
  2.5 2.4 scatter_custom_fusion
  5.6 11.8 %all-to-all-start = ((f32[1,32,16]{2,0,1:T(1,128)}), f32[1,32,16]{2,0,1:T(1,128)}, u32[]{:S(2)}, u32[]{:S(2)}) async-start(f32[1,32,16]{2,0,1:T(1,128)} %bitcast.2), calls=%async_computation | async-start | bytes 32768 | tf_op jit(solution)/shard_map/all_to_all | solution.py:226
  17.4 1.3 copy.739
  20.0 3.0 collective-permute-start.1
  23.8 1.5 collective-permute-start.2
  26.6 1.4 reshape.1350
  35.0 1.6 fusion.10
  40.1 1.2 fusion.2
  52.9 1.3 fusion.82
  54.6 2.3 copy.737
  57.8 3.3 fusion.8
  61.2 1.2 copy.878
  63.8 1.2 copy.875
  67.6 1.6 copy.880
  72.8 1.4 constant_dynamic-update-slice_fusion.306
  74.2 1.5 fusion.84
  76.8 6.4 %scatter-add.26 = f32[5,4,4,4,2,2,128]{6,3,5,4,2,0,1:T(4,128)S(1)} dynamic-update-slice(f32[5,4,4,4,2,2,128]{6,3,5,4,2,0,1:T(4,128)S(1)} %bitcast.649, f32[5,4,4,1,2,2,128]{6,3,5,4,2,0,1:T(1,128)} %multiply_add_fusion, s32[]{:T(128)} %constant.293.clone.1, s32[]{:T(128)} %constant.293.clone.1, s32[]{:T(128)} %constant.293.clone.1, s32[]{:T(128)} %constant.293.clone.1, s32[]{:T(128)} %constant.293.clone.1, ...) | dynamic-update-slice | bytes 327684 | tf_op jit(solution)/shard_map/scatter-add | solution.py:102
  83.2 2.3 fusion.46
  85.4 3.8 scatter_custom_fusion.1
  90.8 1.8 mul.3749
  92.6 1.6 copy.781
  94.2 1.7 stack_reshape.20
  101.8 6.4 %scatter-add.29 = f32[5,4,4,4,2,2,128]{6,3,5,4,2,0,1:T(4,128)S(1)} dynamic-update-slice(f32[5,4,4,4,2,2,128]{6,3,5,4,2,0,1:T(4,128)S(1)} %scatter-add.26, f32[5,4,4,1,2,2,128]{6,3,5,4,2,0,1:T(1,128)} %fusion.46, s32[]{:T(128)} %constant.293.clone.1, s32[]{:T(128)} %constant.293.clone.1, s32[]{:T(128)} %constant.293.clone.1, s32[]{:T(128)} %constant.306.clone.1, s32[]{:T(128)} %constant.293.clone.1, ...) | dynamic-update-slice | bytes 327684 | tf_op jit(solution)/shard_map/scatter-add | solution.py:103
  108.2 75.1 %all-reduce.1 = f32[2048]{0:T(1024)S(1)} all-reduce(f32[2048]{0:T(1024)S(1)} %select_reduce_fusion), channel_id=2, replica_groups=mesh['group'=8,'dev'=32] {'group','dev'}, use_global_device_ids=true, to_apply=%region_10.11.clone | all-reduce | flops 2048 | bytes 16384
  184.0 10.2 %all-to-all-start.1 = ((f32[320,32,16]{0,2,1:T(8,128)}), f32[320,32,16]{0,2,1:T(8,128)}, u32[]{:S(2)}, u32[]{:S(2)}) async-start(f32[320,32,16]{0,2,1:T(8,128)} %bitcast.651), calls=%async_computation.1 | async-start | bytes 1572864 | tf_op jit(solution)/shard_map/all_to_all | solution.py:224
  196.1 1.1 multiply_bitcast_fusion.1
  201.1 1.1 fusion.20
  217.0 2.5 copy.782
  219.5 3.9 scatter_custom_fusion.3
  223.4 9.8 %all-to-all-start.2 = ((f32[480,32,16]{0,2,1:T(8,128)}), f32[480,32,16]{0,2,1:T(8,128)}, u32[]{:S(2)}, u32[]{:S(2)}) async-start(f32[480,32,16]{0,2,1:T(8,128)} %bitcast.45), calls=%async_computation.2 | async-start | bytes 2097152 | tf_op jit(solution)/shard_map/all_to_all | solution.py:225
  233.3 2.9 scatter_custom_fusion.2
  238.0 22.8 %all-to-all-done.2 = f32[480,32,16]{0,2,1:T(8,128)} async-done(((f32[480,32,16]{0,2,1:T(8,128)}), f32[480,32,16]{0,2,1:T(8,128)}, u32[]{:S(2)}, u32[]{:S(2)}) %all-to-all-start.2) | async-done | bytes 983072 | tf_op jit(solution)/shard_map/all_to_all | solution.py:225
  260.8 3.2 scatter_custom_fusion.4
  266.8 1.3 fusion.104
  281.4 1.1 fusion.78
  298.2 1.1 fusion.76
  369.9 1.1 multiply_subtract_fusion
  372.1 2.3 gather_fusion
  374.4 2.2 select_select_fusion
  376.6 5.9 %all-to-all-start.3 = ((f32[320,32,16]{0,2,1:T(8,128)}), f32[320,32,16]{0,2,1:T(8,128)S(1)}, u32[]{:S(2)}, u32[]{:S(2)}) async-start(f32[320,32,16]{0,2,1:T(8,128)} %select_select_fusion), calls=%async_computation.3 | async-start | bytes 1572864 | tf_op jit(solution)/shard_map/all_to_all | solution.py:236
  383.9 1.1 fusion.58
  385.1 1.1 fusion.52
  386.5 17.1 %all-to-all-done.3 = f32[320,32,16]{0,2,1:T(8,128)S(1)} async-done(((f32[320,32,16]{0,2,1:T(8,128)}), f32[320,32,16]{0,2,1:T(8,128)S(1)}, u32[]{:S(2)}, u32[]{:S(2)}) %all-to-all-start.3) | async-done | bytes 655392 | tf_op jit(solution)/shard_map/all_to_all | solution.py:236
  403.6 2.3 gather_fusion.1
  405.9 2.2 copy.839
  408.1 1.6 gather.15
  410.3 1.2 copy.883
  (456 shorter events, 172.3 us)
Async XLA Ops:
  5.6 178.4 %all-to-all-start = ((f32[1,32,16]{2,0,1:T(1,128)}), f32[1,32,16]{2,0,1:T(1,128)}, u32[]{:S(2)}, u32[]{:S(2)}) async-start(f32[1,32,16]{2,0,1:T(1,128)} %bitcast.2), calls=%async_computation | async-start | bytes 32768 | tf_op jit(solution)/shard_map/all_to_all | solution.py:226
  18.7 4.3 %copy-start = (f32[5,4,4,4,2,2,128]{6,5,4,3,2,1,0:T(2,128)S(1)}, f32[5,4,4,4,2,2,128]{6,5,4,3,2,1,0:T(2,128)}, u32[]{:S(2)}) copy-start(f32[5,4,4,4,2,2,128]{6,5,4,3,2,1,0:T(2,128)} %param.17) | copy-start | bytes 1966084
  19.4 176.7 %collective-permute-start = (f32[5,4,4,1,2,128]{5,2,4,3,1,0:T(4,128)}, f32[5,4,4,1,2,128]{5,2,4,3,1,0:T(4,128)}, u32[]{:S(2)}, u32[]{:S(2)}) collective-permute-start(f32[5,4,4,1,2,128]{5,2,4,3,1,0:T(4,128)} %slice.2654), channel_id=1, source_target_pairs={{0,32},{32,64},{64,96},{96,128},{128,160},{160,192},{192,224},{224... | collective-permute-start | bytes 245768 | tf_op jit(solution)/shard_map/ppermute | solution.py:23
  20.0 176.0 %collective-permute-start.1 = (f32[5,4,4,1,2,128]{5,2,4,3,1,0:T(4,128)}, f32[5,4,4,1,2,128]{5,2,4,3,1,0:T(4,128)}, u32[]{:S(2)}, u32[]{:S(2)}) collective-permute-start(f32[5,4,4,1,2,128]{5,2,4,3,1,0:T(4,128)} %slice.2666), channel_id=1, source_target_pairs={{32,0},{64,32},{96,64},{128,96},{160,128},{192,160},{224,192},{0,2... | collective-permute-start | bytes 245768 | tf_op jit(solution)/shard_map/ppermute | solution.py:24
  23.8 180.2 %collective-permute-start.2 = (f32[5,4,4,2,1,128]{5,2,4,3,0,1:T(4,128)}, f32[5,4,4,2,1,128]{5,2,4,3,0,1:T(4,128)S(1)}, u32[]{:S(2)}, u32[]{:S(2)}) collective-permute-start(f32[5,4,4,2,1,128]{5,2,4,3,0,1:T(4,128)} %slice.2679), channel_id=1, source_target_pairs={{0,1},{1,2},{2,3},{3,4},{4,5},{5,6},{6,7},{7,8},{8,9},{9,10},{10,1... | collective-permute-start | bytes 245768 | tf_op jit(solution)/shard_map/ppermute | solution.py:23
  25.9 178.0 %collective-permute-start.3 = (f32[5,4,4,2,1,128]{5,2,4,3,0,1:T(4,128)}, f32[5,4,4,2,1,128]{5,2,4,3,0,1:T(4,128)}, u32[]{:S(2)}, u32[]{:S(2)}) collective-permute-start(f32[5,4,4,2,1,128]{5,2,4,3,0,1:T(4,128)} %slice.2690), channel_id=1, source_target_pairs={{1,0},{2,1},{3,2},{4,3},{5,4},{6,5},{7,6},{8,7},{9,8},{10,9},{11,1... | collective-permute-start | bytes 245768 | tf_op jit(solution)/shard_map/ppermute | solution.py:24
  28.2 1.5 copy-start.11
  28.3 1.4 copy-start.30
  35.0 1.6 copy-start.6
  36.6 0.8 copy-start.4
  37.4 0.9 copy-start.12
  37.4 0.9 copy-start.31
  40.0 1.3 copy-start.8
  40.1 1.3 copy-start.9
  42.1 0.9 copy-start.36
  43.1 0.9 copy-start.35
  44.2 0.9 copy-start.17
  44.3 1.7 copy-start.28
  52.0 0.9 copy-start.32
  54.1 2.8 copy-start.13
  54.6 2.3 copy-start.18
  56.9 0.9 copy-start.39
  61.2 1.2 copy-start.33
  62.4 0.9 copy-start.22
  63.3 1.7 copy-start.34
  65.6 1.3 copy-start.23
  67.0 2.3 slice-start.1
  67.6 8.1 %copy-start.10 = (f32[5,4,4,4,2,2,128]{6,3,5,4,2,0,1:T(4,128)S(1)}, f32[5,4,4,4,2,2,128]{6,3,5,4,2,0,1:T(4,128)}, u32[]{:S(2)}) copy-start(f32[5,4,4,4,2,2,128]{6,3,5,4,2,0,1:T(4,128)} %copy-done.9) | copy-start | bytes 1966084
  74.2 1.5 copy-start.20
  85.4 3.8 copy-start.19
  89.3 0.8 copy-start.29
  90.8 9.8 %copy-start.5 = (f32[5,4,4,2,2,128,4]{5,6,4,3,2,1,0:T(4,128)S(1)}, f32[5,4,4,2,2,128,4]{5,6,4,3,2,1,0:T(4,128)}, u32[]{:S(2)}) copy-start(f32[5,4,4,2,2,128,4]{5,6,4,3,2,1,0:T(4,128)} %fusion.8) | copy-start | bytes 1966084
  94.2 1.7 copy-start.40
  100.8 0.9 copy-start.3
  108.2 75.8 %copy-start.1 = (f32[5,4,4,4,2,2,128]{6,3,5,4,2,0,1:T(4,128)}, f32[5,4,4,4,2,2,128]{6,3,5,4,2,0,1:T(4,128)S(1)}, u32[]{:S(2)}) copy-start(f32[5,4,4,4,2,2,128]{6,3,5,4,2,0,1:T(4,128)S(1)} %scatter-add.29) | copy-start | bytes 1966084
  184.0 39.5 %all-to-all-start.1 = ((f32[320,32,16]{0,2,1:T(8,128)}), f32[320,32,16]{0,2,1:T(8,128)}, u32[]{:S(2)}, u32[]{:S(2)}) async-start(f32[320,32,16]{0,2,1:T(8,128)} %bitcast.651), calls=%async_computation.1 | async-start | bytes 1572864 | tf_op jit(solution)/shard_map/all_to_all | solution.py:224
  195.9 37.4 %copy-start.44 = (s32[512,1]{0,1:T(1,128)}, s32[512,1]{0,1:T(1,128)S(1)}, u32[]{:S(2)}) copy-start(s32[512,1]{0,1:T(1,128)S(1)} %get-tuple-element.477) | copy-start | bytes 6148
  211.2 1.1 copy-start.24
  213.6 1.4 copy-start.27
  214.3 1.0 copy-start.25
  214.3 1.1 copy-start.26
  215.4 0.9 copy-start.21
  223.4 37.4 %all-to-all-start.2 = ((f32[480,32,16]{0,2,1:T(8,128)}), f32[480,32,16]{0,2,1:T(8,128)}, u32[]{:S(2)}, u32[]{:S(2)}) async-start(f32[480,32,16]{0,2,1:T(8,128)} %bitcast.45), calls=%async_computation.2 | async-start | bytes 2097152 | tf_op jit(solution)/shard_map/all_to_all | solution.py:225
  376.6 27.0 %all-to-all-start.3 = ((f32[320,32,16]{0,2,1:T(8,128)}), f32[320,32,16]{0,2,1:T(8,128)S(1)}, u32[]{:S(2)}, u32[]{:S(2)}) async-start(f32[320,32,16]{0,2,1:T(8,128)} %select_select_fusion), calls=%async_computation.3 | async-start | bytes 1572864 | tf_op jit(solution)/shard_map/all_to_all | solution.py:236
  383.9 2.3 copy-start.7
  385.1 1.2 slice-start
  385.1 1.2 copy-start.15
  408.1 1.6 copy-start.2
  (7 other events, 4.7 us)
where the time goes:
time: 419 us; the launch traced here: 412 us
  other arithmetic  146 us (35%)
  local copies, waits for them, and re-layouts  99.4 us (24%)
  blocking collectives  75.1 us (18%)
  starting transfers between devices  42.8 us (10%)
  waiting for transfers between devices  39.9 us (10%)
  matrix products  6.16 us (1%)
    unnamed x1, blocking collectives  75.1 us
    unnamed x142, other arithmetic  62.8 us
    sub x29, other arithmetic, rusanov(): 0.5 * (left_flux + right_flux) - 0.5 * fastest * (right_state - left_state)  25.8 us
    another operation x49, other arithmetic, euler_flux(): return (jnp.stack(flux_rows), wave_speed)  23.7 us
    all_to_all x1, waiting for transfers between devices, on_device(): lax.all_to_all(send_flux, 'dev', split_axis=1, concat_axis=1, tiled=True)  22.8 us
    unnamed x112, local copies, waits for them, and re-layouts  19.2 us
    all_to_all x1, waiting for transfers between devices, on_device(): lax.all_to_all(answers, 'dev', split_axis=1, concat_axis=1, tiled=True)  17.1 us
    mul x26, other arithmetic, rusanov(): 0.5 * fastest * (right_state - left_state)  14.5 us
  transfers between devices with their start and end apart: 8, of which 2 were waited for; matrix products, arithmetic and copies ran while one was open for 28% of the time, Pallas kernels for 0%

commit v1 on v0

v1 whole, which is shorter than its diff:
```python
import jax
import jax.numpy as jnp
import numpy as np
from jax import lax
from jax.experimental import pallas as pl
from jax.experimental.pallas import tpu as pltpu
from jax.sharding import PartitionSpec as P

SUBSTEPS = 8
SN_DEV = 8
GAMMA = 1.4
COURANT = 0.02
F32 = jnp.float32

ROWS = 1280


def blk(v, i, j, h):
    return (((v * 4 + i) * 4 + j) * 2 + h) * 8


def nod(q, i, j, h):
    return q * 256 + ((i * 4 + j) * 2 + h) * 8


FLUX_OF = (
    (None, 0, 1, 2, 6),
    (None, 1, 3, 4, 7),
    (None, 2, 4, 5, 8),
)


def derivative_table():
    gll_nodes = np.array([-1.0, -np.sqrt(0.2), np.sqrt(0.2), 1.0])
    bary = np.array(
        [1.0 / np.prod([gll_nodes[a] - gll_nodes[b] for b in range(4) if b != a]) for a in range(4)]
    )
    table = np.zeros((4, 4))
    for a in range(4):
        for b in range(4):
            if a != b:
                table[a, b] = bary[b] / bary[a] / (gll_nodes[a] - gll_nodes[b])
    for a in (0, 3):
        table[a, a] = -np.sum(table[a])
    return table


WEIGHTS = np.array([1.0, 5.0, 5.0, 1.0]) / 6.0


def row_bit(bit):
    rows = lax.broadcasted_iota(jnp.int32, (8, 128), 0)
    return (rows & bit) != 0


def turn(x, shift):
    return pltpu.roll(x, shift % 8, 0)


def point_flux(u, d):
    inv = 1.0 / u[0]
    v = u[1 + d] * inv
    ke = (u[1] * u[1] + u[2] * u[2] + u[3] * u[3]) * inv
    p = (GAMMA - 1.0) * (u[4] - 0.5 * ke)
    flux = [u[1 + d]] + [u[1 + a] * v for a in range(3)] + [v * (u[4] + p)]
    flux[1 + d] = flux[1 + d] + p
    speed = jnp.abs(v) + jnp.sqrt(GAMMA * p * inv)
    return flux, speed


def twice_face(fl, fr, s, ul, ur):
    return (fl + fr) - s * (ur - ul)


def z_wall_pair(own, lane):
    low = jnp.logical_not(row_bit(4))
    wall = (low & (lane == 0)) | (row_bit(4) & (lane == 127))
    across = []
    for c in range(5):
        x = turn(own[c], 4)
        n = jnp.where(low, pltpu.roll(x, 1, 1), pltpu.roll(x, 127, 1))
        across.append(jnp.where(wall, -own[c] if c == 3 else own[c], n))
    return across


def prepare_kernel(s_ref, own_ref, xl_ref, xh_ref, yl_ref, yh_ref, part_ref):
    bx, by, bk = row_bit(2), row_bit(1), row_bit(4)
    lane = lax.broadcasted_iota(jnp.int32, (8, 128), 1)

    def get(v, i, j, h):
        return s_ref[pl.ds(blk(v, i, j, h), 8), :]

    for c in range(5):
        for a in range(4):
            row = pl.ds((c * 4 + a) * 8, 8)
            xl_ref[row, :] = jnp.where(bx, get(c, 3, a, 1), turn(get(c, 3, a, 0), -2))
            xh_ref[row, :] = jnp.where(bx, turn(get(c, 0, a, 0), 2), get(c, 0, a, 1))
            yl_ref[row, :] = jnp.where(by, get(c, a, 3, 1), turn(get(c, a, 3, 0), -1))
            yh_ref[row, :] = jnp.where(by, turn(get(c, a, 0, 0), 1), get(c, a, 0, 1))

    total = jnp.zeros((8, 128), F32)
    sign = jnp.where(bk, 0.5, -0.5).astype(F32)
    for i in range(4):
        for j in range(4):
            own = [jnp.where(bk, get(c, i, j, 1), get(c, i, j, 0)) for c in range(5)]
            across = list(own)
            across[3] = -own[3]
            fo, so = point_flux(own, 2)
            fa, sa = point_flux(across, 2)
            jump = jnp.where(bk, across[3] - own[3], own[3] - across[3])
            flux = (fo[3] + fa[3]) - jnp.maximum(so, sa) * jump
            total = total + float(WEIGHTS[i] * WEIGHTS[j]) * flux
    at_wall = (bk & (lane == 127)) | (jnp.logical_not(bk) & (lane == 0))
    loads = jnp.sum(jnp.where(at_wall, total * sign, 0.0), axis=1, keepdims=True)
    part_ref[...] = jnp.zeros(part_ref.shape, F32)
    lane1 = lax.broadcasted_iota(jnp.int32, (1, 128), 1)
    for side in range(2):
        for x in range(2):
            for y in range(2):
                node = own_ref[x, y, side]
                r = side * 4 + x * 2 + y
                at = pl.ds(node // SN_DEV, 1)
                part_ref[at, :] = part_ref[at, :] + jnp.where(
                    lane1 == node % SN_DEV, loads[r : r + 1, :], 0.0
                )


def section_kernel(
    s_ref, slot_ref, xl_ref, xh_ref, yl_ref, yh_ref, out_ref,
    u_ref, f_ref, s3_ref, sm_ref, gx_ref, gy_ref, gz_ref,
):
    bx, by, bk = row_bit(2), row_bit(1), row_bit(4)
    low = jnp.logical_not(bk)
    lane = lax.broadcasted_iota(jnp.int32, (8, 128), 1)
    IJ = [(i, j) for i in range(4) for j in range(4)]

    def nodal(src):
        for i, j in IJ:
            for h in range(2):
                u = [src[pl.ds(blk(c, i, j, h), 8), :] for c in range(5)]
                inv = 1.0 / u[0]
                v = [u[1 + d] * inv for d in range(3)]
                xx, xy, xz = u[1] * v[0], u[1] * v[1], u[1] * v[2]
                yy, yz, zz = u[2] * v[1], u[2] * v[2], u[3] * v[2]
                p = (GAMMA - 1.0) * (u[4] - 0.5 * (xx + yy + zz))
                e = u[4] + p
                sound = jnp.sqrt(GAMMA * p * inv)
                q = [xx + p, xy, xz, yy + p, yz, zz + p, v[0] * e, v[1] * e, v[2] * e]
                for n in range(9):
                    f_ref[pl.ds(nod(n, i, j, h), 8), :] = q[n]
                for d in range(3):
                    s3_ref[pl.ds(nod(d, i, j, h), 8), :] = jnp.abs(v[d]) + sound
        for a in range(3):
            for b in range(4):
                for h in range(2):
                    sm_ref[pl.ds(nod(0, a, b, h), 8), :] = jnp.maximum(
                        s3_ref[pl.ds(nod(0, a, b, h), 8), :], s3_ref[pl.ds(nod(0, a + 1, b, h), 8), :]
                    )
                    sm_ref[pl.ds(nod(1, b, a, h), 8), :] = jnp.maximum(
                        s3_ref[pl.ds(nod(1, b, a, h), 8), :], s3_ref[pl.ds(nod(1, b, a + 1, h), 8), :]
                    )
        for i, j in IJ:
            mid = s3_ref[pl.ds(nod(2, i, j, 0) + 4, 8), :]
            for h in range(2):
                sm_ref[pl.ds(nod(2, i, j, h), 8), :] = jnp.maximum(
                    s3_ref[pl.ds(nod(2, i, j, h), 8), :], mid
                )

    def flux(src, d, c, i, j, h, off=0):
        if c == 0:
            return src[pl.ds(blk(1 + d, i, j, h) + off, 8), :]
        return f_ref[pl.ds(nod(FLUX_OF[d][c], i, j, h) + off, 8), :]

    def cell(src, c, i, j, h, off=0):
        return src[pl.ds(blk(c, i, j, h) + off, 8), :]

    nodal(s_ref)
    for b in range(4):
        for h in range(2):
            for d, g_ref, lo_ref, hi_ref, bit, step in (
                (0, gx_ref, xl_ref, xh_ref, bx, 2),
                (1, gy_ref, yl_ref, yh_ref, by, 1),
            ):
                first = (0, b) if d == 0 else (b, 0)
                last = (3, b) if d == 0 else (b, 3)
                uf = [cell(s_ref, c, *first, h) for c in range(5)]
                ul = [cell(s_ref, c, *last, h) for c in range(5)]
                hl = [lo_ref[pl.ds((c * 4 + b) * 8, 8), :] for c in range(5)]
                hh = [hi_ref[pl.ds((c * 4 + b) * 8, 8), :] for c in range(5)]
                if h == 1:
                    hl = [turn(t, -step) for t in hl]
                    hh = [turn(t, step) for t in hh]
                before = [jnp.where(bit, turn(ul[c], step), hl[c]) for c in range(5)]
                after = [jnp.where(bit, hh[c], turn(uf[c], -step)) for c in range(5)]
                fb, sb = point_flux(before, d)
                fa, sa = point_flux(after, d)
                sl = jnp.maximum(sb, s3_ref[pl.ds(nod(d, *first, h), 8), :])
                sh = jnp.maximum(sa, s3_ref[pl.ds(nod(d, *last, h), 8), :])
                for c in range(5):
                    at = ((c * 4 + b) * 2 + h) * 8
                    g_ref[pl.ds(at, 8), :] = twice_face(
                        fb[c], flux(s_ref, d, c, *first, h), sl, before[c], uf[c]
                    )
                    g_ref[pl.ds(320 + at, 8), :] = twice_face(
                        flux(s_ref, d, c, *last, h), fa[c], sh, ul[c], after[c]
                    )
    for i, j in IJ:
        own = [jnp.where(bk, cell(s_ref, c, i, j, 1), cell(s_ref, c, i, j, 0)) for c in range(5)]
        across = z_wall_pair(own, lane)
        fo, so = point_flux(own, 2)
        fa, sa = point_flux(across, 2)
        s = jnp.maximum(so, sa)
        s = jnp.where(bk, s, -s)
        for c in range(5):
            gz_ref[pl.ds(((c * 4 + i) * 4 + j) * 8, 8), :] = (fo[c] + fa[c]) - s * (across[c] - own[c])

    def gxy(g_ref, side, c, b, h):
        return g_ref[pl.ds(side * 320 + ((c * 4 + b) * 2 + h) * 8, 8), :]

    def gz(c, i, j):
        return gz_ref[pl.ds(((c * 4 + i) * 4 + j) * 8, 8), :]

    table = derivative_table()
    table[0, 0] += 1.0 / WEIGHTS[0]
    table[3, 3] -= 1.0 / WEIGHTS[3]
    table = COURANT * table
    lift = COURANT * 0.5 / WEIGHTS[0]

    def lanes_pair(lo_value, hi_value):
        return jnp.where(bk, float(hi_value), float(lo_value)).astype(F32)

    zc = [
        [lanes_pair(table[2 * h, 2 * g], table[2 * h + 1, 2 * g + 1]) for g in range(2)]
        + [lanes_pair(table[2 * h, 2 * g + 1], table[2 * h + 1, 2 * g]) for g in range(2)]
        for h in range(2)
    ]
    zl = [lanes_pair(-lift, 0.0), lanes_pair(0.0, lift)]

    for c in range(5):
        for h in range(2):
            acc = {}
            for b in range(4):
                for d in range(2):
                    line = [(a, b) if d == 0 else (b, a) for a in range(4)]
                    fl = [flux(s_ref, d, c, *n, h) for n in line]
                    g_ref = gx_ref if d == 0 else gy_ref
                    for a in range(4):
                        r = None
                        for m in range(4):
                            if table[a, m] != 0.0:
                                t = float(table[a, m]) * fl[m]
                                r = t if r is None else r + t
                        if a == 0:
                            r = r - float(lift) * gxy(g_ref, 0, c, b, h)
                        if a == 3:
                            r = r + float(lift) * gxy(g_ref, 1, c, b, h)
                        acc.setdefault(line[a], []).append(r)
            for i, j in IJ:
                fa = flux(s_ref, 2, c, i, j, 0)
                fb = flux(s_ref, 2, c, i, j, 1)
                r = zc[h][0] * fa + zc[h][1] * fb + zc[h][2] * turn(fa, 4) + zc[h][3] * turn(fb, 4)
                r = r + zl[h] * gz(c, i, j)
                r = r + (acc[i, j][0] + acc[i, j][1])
                out_ref[pl.ds(blk(c, i, j, h), 8), :] = cell(s_ref, c, i, j, h) - r

    scale = COURANT / SUBSTEPS * 0.5 / WEIGHTS
    kz = [lanes_pair(scale[0], scale[1]), lanes_pair(scale[2], scale[3])]

    def advance(src, put):
        for c in range(5):
            done = {}
            for h in range(2):
                diff = {}
                for b in range(4):
                    for d in range(2):
                        line = [(a, b) if d == 0 else (b, a) for a in range(4)]
                        g_ref = gx_ref if d == 0 else gy_ref
                        u = [cell(src, c, *n, h) for n in line]
                        f = [flux(src, d, c, *n, h) for n in line]
                        g = [gxy(g_ref, 0, c, b, h)]
                        for a in range(3):
                            g.append(
                                twice_face(
                                    f[a], f[a + 1],
                                    sm_ref[pl.ds(nod(d, *line[a], h), 8), :],
                                    u[a], u[a + 1],
                                )
                            )
                        g.append(gxy(g_ref, 1, c, b, h))
                        for a in range(4):
                            diff[d, line[a]] = g[a + 1] - g[a]
                for i, j in IJ:
                    if scale[i] == scale[j]:
                        r = float(scale[i]) * (diff[0, (i, j)] + diff[1, (i, j)])
                    else:
                        r = float(scale[i]) * diff[0, (i, j)] + float(scale[j]) * diff[1, (i, j)]
                    u = cell(src, c, i, j, h)
                    um = cell(src, c, i, j, 0, 4)
                    fz = flux(src, 2, c, i, j, h)
                    fm = flux(src, 2, c, i, j, 0, 4)
                    s = sm_ref[pl.ds(nod(2, i, j, h), 8), :]
                    if h == 0:
                        t = twice_face(fz, fm, s, u, um)
                        dz = t - jnp.where(low, gz(c, i, j), turn(t, 4))
                    else:
                        t = twice_face(fm, fz, s, um, u)
                        dz = jnp.where(low, turn(t, 4), gz(c, i, j)) - t
                    done[i, j, h] = u - (r + kz[h] * dz)
            for (i, j, h), value in done.items():
                put(c, i, j, h, value)

    def put_u(c, i, j, h, value):
        u_ref[pl.ds(blk(c, i, j, h), 8), :] = value

    def put_out(c, i, j, h, value):
        at = pl.ds(blk(c, i, j, h), 8)
        out_ref[at, :] = jnp.where(troubled, value, out_ref[at, :])

    u_ref[...] = s_ref[...]

    def substep(_, carry):
        advance(u_ref, put_u)
        nodal(u_ref)
        return carry

    lax.fori_loop(0, SUBSTEPS - 1, substep, 0)
    slot = slot_ref[...]
    troubled = jnp.concatenate([slot, slot], axis=0) >= 0
    advance(u_ref, put_out)


def on_device(state, limit_slot, wall_owner, interpret=False):
    n_group, n_dev = lax.axis_size("group"), lax.axis_size("dev")
    devices = n_group * n_dev
    rows = state.reshape(ROWS, 128)
    halo = jax.ShapeDtypeStruct((160, 128), F32)
    vmem = pl.BlockSpec(memory_space=pltpu.VMEM)
    xl, xh, yl, yh, part = pl.pallas_call(
        prepare_kernel,
        out_shape=(halo, halo, halo, halo, jax.ShapeDtypeStruct((devices, 128), F32)),
        in_specs=[vmem, pl.BlockSpec(memory_space=pltpu.SMEM)],
        out_specs=(vmem,) * 5,
        name="prepare",
        interpret=interpret,
    )(rows, wall_owner)

    def shift(x, axis, by):
        n = lax.axis_size(axis)
        return lax.ppermute(x, axis, [(i, (i + by) % n) for i in range(n)])

    xl, xh = shift(xl, "group", 1), shift(xh, "group", -1)
    yl, yh = shift(yl, "dev", 1), shift(yh, "dev", -1)
    parts = lax.all_to_all(part, ("group", "dev"), 0, 0, tiled=True)
    wall_loads = jnp.sum(parts[:, :SN_DEV], axis=0)
    out = pl.pallas_call(
        section_kernel,
        out_shape=jax.ShapeDtypeStruct((ROWS, 128), F32),
        in_specs=[vmem] * 6,
        out_specs=vmem,
        scratch_shapes=[
            pltpu.VMEM((ROWS, 128), F32),
            pltpu.VMEM((9 * 256, 128), F32),
            pltpu.VMEM((3 * 256, 128), F32),
            pltpu.VMEM((3 * 256, 128), F32),
            pltpu.VMEM((640, 128), F32),
            pltpu.VMEM((640, 128), F32),
            pltpu.VMEM((640, 128), F32),
        ],
        cost_estimate=pl.CostEstimate(flops=60_000_000, transcendentals=600_000, bytes_accessed=2_000_000),
        name="section",
        interpret=interpret,
    )(rows, limit_slot.reshape(4, 128), xl, xh, yl, yh)
    return out.reshape(state.shape), wall_loads


def solution(mesh):
    in_specs = (
        P(None, None, None, None, "group", "dev", None),
        P("group", "dev", None),
        P("group", "dev", None),
    )
    out_specs = (P(None, None, None, None, "group", "dev", None), P(("group", "dev")))
    return jax.shard_map(
        on_device, mesh=mesh, in_specs=in_specs, out_specs=out_specs, check_vma=False
    )
```

time: 419 us -> 39.9 us (0.10)
  the two profiles are of different devices: /device:TPU:8 before, /device:TPU:120 now
where the time goes in v1:
time: 39.9 us; the launch traced here: 39.7 us
  starting transfers between devices  19.6 us (49%)
  Pallas kernels  10.6 us (27%)
  waiting for transfers between devices  7.73 us (19%)
  between operations  0.68 us (2%)
  local copies, waits for them, and re-layouts  0.63 us (2%)
  other arithmetic  0.56 us (1%)
    all_to_all x1, starting transfers between devices, on_device(): parts = lax.all_to_all(part, ('group', 'dev'), 0, 0, tiled=True)  13.9 us
    pallas_call x1, Pallas kernels, on_device(): pl.pallas_call(section_kernel, out_shape=jax.ShapeDtypeStruct((ROWS, 128)...  8.56 us
    ppermute x4, waiting for transfers between devices, shift(): return lax.ppermute(x, axis, [(i, (i + by) % n) for i in range(n)])  7.72 us
    ppermute x4, starting transfers between devices, shift(): return lax.ppermute(x, axis, [(i, (i + by) % n) for i in range(n)])  5.71 us
    pallas_call x1, Pallas kernels, on_device(): pl.pallas_call(prepare_kernel, out_shape=(halo, halo, halo, halo, jax.Sha...  1.99 us
  transfers between devices with their start and end apart: 5, of which 2 were waited for; matrix products, arithmetic and copies ran while one was open for 0% of the time, Pallas kernels for 22%

profile of v1, /device:TPU:120, one launch (start us, length us, event | category | flops | bytes accessed | tf_op | source)
XLA Modules:
  0.0 39.7 jit_solution(2565195113501638745)
XLA Ops:
  0.6 2.0 %prepare.1 = (f32[160,128]{1,0:T(8,128)}, f32[160,128]{1,0:T(8,128)}, f32[160,128]{1,0:T(8,128)}, f32[160,128]{1,0:T(8,128)}, f32[256,128]{1,0:T(8,128)}) custom-call(f32[1280,128]{1,0:T(8,128)} %bitcast.7, s32[2,2,2]{2,1,0:T(2,128)} %own_ref.1), custom_call_target="tpu_custom_call" | custom-call | tf_op jit(solution)/shard_map/prepare/pallas_call | solution.py:338
  2.6 0.0 copy-start.6
  2.6 0.0 copy-start.5
  2.6 0.0 copy-start.4
  2.6 13.9 %all-to-all-start = ((f32[256,1,128]{2,1,0:T(1,128)}), f32[256,1,128]{2,1,0:T(1,128)S(1)}, u32[]{:S(2)}, u32[]{:S(2)}) async-start(f32[256,1,128]{2,1,0:T(1,128)} %bitcast.11), calls=%async_computation | async-start | bytes 262144 | tf_op jit(solution)/shard_map/all_to_all | solution.py:353
  16.5 0.1 collective-permute-start
  16.7 0.0 copy-done.6
  16.7 2.8 %collective-permute-start.1 = (f32[160,128]{1,0:T(8,128)S(1)}, f32[160,128]{1,0:T(8,128)S(1)}, u32[]{:S(2)}, u32[]{:S(2)}) collective-permute-start(f32[160,128]{1,0:T(8,128)S(1)} %copy-done.6), channel_id=1, source_target_pairs={{0,224},{32,0},{64,32},{96,64},{128,96},{160,128},{192,160},{224,1... | collective-permute-start | bytes 245768 | tf_op jit(solution)/shard_map/ppermute | solution.py:349
  19.5 0.0 copy-done.5
  19.5 2.7 %collective-permute-start.2 = (f32[160,128]{1,0:T(8,128)S(1)}, f32[160,128]{1,0:T(8,128)S(1)}, u32[]{:S(2)}, u32[]{:S(2)}) collective-permute-start(f32[160,128]{1,0:T(8,128)S(1)} %copy-done.5), channel_id=1, source_target_pairs={{0,1},{1,2},{2,3},{3,4},{4,5},{5,6},{6,7},{7,8},{8,9},{9,10},{10,1... | collective-permute-start | bytes 245768 | tf_op jit(solution)/shard_map/ppermute | solution.py:349
  22.2 0.0 copy-done.4
  22.2 0.0 collective-permute-start.3
  22.2 0.0 collective-permute-done.xl_ref
  22.2 0.0 copy-start
  22.3 0.0 collective-permute-done.1.xh_ref
  22.3 0.0 copy-start.1
  22.3 2.0 %collective-permute-done.2.yl_ref = f32[160,128]{1,0:T(8,128)S(1)} collective-permute-done((f32[160,128]{1,0:T(8,128)S(1)}, f32[160,128]{1,0:T(8,128)S(1)}, u32[]{:S(2)}, u32[]{:S(2)}) %collective-permute-start.2) | collective-permute-done | bytes 81952 | tf_op jit(solution)/shard_map/ppermute | solution.py:349
  24.3 0.0 copy-start.2
  24.3 5.7 %collective-permute-done.3.yh_ref = f32[160,128]{1,0:T(8,128)S(1)} collective-permute-done((f32[160,128]{1,0:T(8,128)S(1)}, f32[160,128]{1,0:T(8,128)S(1)}, u32[]{:S(2)}, u32[]{:S(2)}) %collective-permute-start.3) | collective-permute-done | bytes 81952 | tf_op jit(solution)/shard_map/ppermute | solution.py:349
  30.0 0.0 copy-start.3
  30.0 0.0 copy-done
  30.0 0.0 copy-done.1
  30.0 0.0 copy-done.2
  30.0 0.6 %copy-done.3 = f32[160,128]{1,0:T(8,128)} copy-done((f32[160,128]{1,0:T(8,128)}, f32[160,128]{1,0:T(8,128)S(1)}, u32[]{:S(2)}) %copy-start.3) | copy-done | bytes 81944
  30.6 8.6 %section.1 = f32[1280,128]{1,0:T(8,128)} custom-call(f32[1280,128]{1,0:T(8,128)} %bitcast.8, s32[4,128]{1,0:T(4,128)} %bitcast.12, f32[160,128]{1,0:T(8,128)} %copy-done, f32[160,128]{1,0:T(8,128)} %copy-done.1, f32[160,128]{1,0:T(8,128)} %copy-done.2, f32[160,128]{1,0:T(8,128)} %copy-done.3), custom_call_target="tpu_custom_call" | custom-call | flops 60000000 | bytes 2000000 | tf_op jit(solution)/shard_map/section/pallas_call | solution.py:355
  39.2 0.0 all-to-all-done
  39.2 0.6 %slice_reduce_fusion = f32[8]{0:T(128)} fusion(f32[256,128]{1,0:T(8,128)S(1)} %bitcast.10), kind=kLoop, calls=%fused_computation | loop fusion | flops 2040 | bytes 8224 | tf_op jit(solution)/shard_map/reduce_sum | solution.py:354
Async XLA Ops:
  2.6 14.0 %copy-start.6 = (f32[160,128]{1,0:T(8,128)S(1)}, f32[160,128]{1,0:T(8,128)}, u32[]{:S(2)}) copy-start(f32[160,128]{1,0:T(8,128)} %get-tuple-element.8) | copy-start | bytes 245764
  2.6 16.9 %copy-start.5 = (f32[160,128]{1,0:T(8,128)S(1)}, f32[160,128]{1,0:T(8,128)}, u32[]{:S(2)}) copy-start(f32[160,128]{1,0:T(8,128)} %get-tuple-element.9) | copy-start | bytes 245764
  2.6 19.6 %copy-start.4 = (f32[160,128]{1,0:T(8,128)S(1)}, f32[160,128]{1,0:T(8,128)}, u32[]{:S(2)}) copy-start(f32[160,128]{1,0:T(8,128)} %get-tuple-element.10) | copy-start | bytes 245764
  2.6 36.6 %all-to-all-start = ((f32[256,1,128]{2,1,0:T(1,128)}), f32[256,1,128]{2,1,0:T(1,128)S(1)}, u32[]{:S(2)}, u32[]{:S(2)}) async-start(f32[256,1,128]{2,1,0:T(1,128)} %bitcast.11), calls=%async_computation | async-start | bytes 262144 | tf_op jit(solution)/shard_map/all_to_all | solution.py:353
  16.5 5.7 %collective-permute-start = (f32[160,128]{1,0:T(8,128)}, f32[160,128]{1,0:T(8,128)S(1)}, u32[]{:S(2)}, u32[]{:S(2)}) collective-permute-start(f32[160,128]{1,0:T(8,128)} %get-tuple-element.7), channel_id=1, source_target_pairs={{0,32},{32,64},{64,96},{96,128},{128,160},{160,192},{192,224},{224... | collective-permute-start | bytes 245768 | tf_op jit(solution)/shard_map/ppermute | solution.py:349
  16.7 5.6 %collective-permute-start.1 = (f32[160,128]{1,0:T(8,128)S(1)}, f32[160,128]{1,0:T(8,128)S(1)}, u32[]{:S(2)}, u32[]{:S(2)}) collective-permute-start(f32[160,128]{1,0:T(8,128)S(1)} %copy-done.6), channel_id=1, source_target_pairs={{0,224},{32,0},{64,32},{96,64},{128,96},{160,128},{192,160},{224,1... | collective-permute-start | bytes 245768 | tf_op jit(solution)/shard_map/ppermute | solution.py:349
  19.5 4.8 %collective-permute-start.2 = (f32[160,128]{1,0:T(8,128)S(1)}, f32[160,128]{1,0:T(8,128)S(1)}, u32[]{:S(2)}, u32[]{:S(2)}) collective-permute-start(f32[160,128]{1,0:T(8,128)S(1)} %copy-done.5), channel_id=1, source_target_pairs={{0,1},{1,2},{2,3},{3,4},{4,5},{5,6},{6,7},{7,8},{8,9},{9,10},{10,1... | collective-permute-start | bytes 245768 | tf_op jit(solution)/shard_map/ppermute | solution.py:349
  22.2 7.8 %collective-permute-start.3 = (f32[160,128]{1,0:T(8,128)S(1)}, f32[160,128]{1,0:T(8,128)S(1)}, u32[]{:S(2)}, u32[]{:S(2)}) collective-permute-start(f32[160,128]{1,0:T(8,128)S(1)} %copy-done.4), channel_id=1, source_target_pairs={{0,31},{1,0},{2,1},{3,2},{4,3},{5,4},{6,5},{7,6},{8,7},{9,8},{10,9... | collective-permute-start | bytes 245768 | tf_op jit(solution)/shard_map/ppermute | solution.py:349
  22.2 7.8 %copy-start = (f32[160,128]{1,0:T(8,128)}, f32[160,128]{1,0:T(8,128)S(1)}, u32[]{:S(2)}) copy-start(f32[160,128]{1,0:T(8,128)S(1)} %collective-permute-done.xl_ref) | copy-start | bytes 245764
  22.3 7.7 %copy-start.1 = (f32[160,128]{1,0:T(8,128)}, f32[160,128]{1,0:T(8,128)S(1)}, u32[]{:S(2)}) copy-start(f32[160,128]{1,0:T(8,128)S(1)} %collective-permute-done.1.xh_ref) | copy-start | bytes 245764
  24.3 5.7 %copy-start.2 = (f32[160,128]{1,0:T(8,128)}, f32[160,128]{1,0:T(8,128)S(1)}, u32[]{:S(2)}) copy-start(f32[160,128]{1,0:T(8,128)S(1)} %collective-permute-done.2.yl_ref) | copy-start | bytes 245764
  30.0 0.6 %copy-start.3 = (f32[160,128]{1,0:T(8,128)}, f32[160,128]{1,0:T(8,128)S(1)}, u32[]{:S(2)}) copy-start(f32[160,128]{1,0:T(8,128)S(1)} %collective-permute-done.3.yh_ref) | copy-start | bytes 245764

commit v2 on v1

--- a/solution.py
+++ b/solution.py
@@ -6,6 +6,7 @@
 from jax.experimental.pallas import tpu as pltpu
 from jax.sharding import PartitionSpec as P
 
+
 SUBSTEPS = 8
 SN_DEV = 8
 GAMMA = 1.4
@@ -13,6 +14,7 @@
 F32 = jnp.float32
 
 ROWS = 1280
+VMEM_LIMIT = 16 * 1024 * 1024
 
 
 def blk(v, i, j, h):
@@ -83,20 +85,29 @@
     return across
 
 
-def prepare_kernel(s_ref, own_ref, xl_ref, xh_ref, yl_ref, yh_ref, part_ref):
+def parity(axis):
+    return jnp.full((8, 128), lax.axis_index(axis) % 2, jnp.int32) == 0
+
+
+def prepare_kernel(s_ref, own_ref, ye_ref, yo_ref, xe_ref, xo_ref, part_ref):
     bx, by, bk = row_bit(2), row_bit(1), row_bit(4)
     lane = lax.broadcasted_iota(jnp.int32, (8, 128), 1)
 
     def get(v, i, j, h):
         return s_ref[pl.ds(blk(v, i, j, h), 8), :]
 
+    ex, ey = parity("group"), parity("dev")
     for c in range(5):
         for a in range(4):
             row = pl.ds((c * 4 + a) * 8, 8)
-            xl_ref[row, :] = jnp.where(bx, get(c, 3, a, 1), turn(get(c, 3, a, 0), -2))
-            xh_ref[row, :] = jnp.where(bx, turn(get(c, 0, a, 0), 2), get(c, 0, a, 1))
-            yl_ref[row, :] = jnp.where(by, get(c, a, 3, 1), turn(get(c, a, 3, 0), -1))
-            yh_ref[row, :] = jnp.where(by, turn(get(c, a, 0, 0), 1), get(c, a, 0, 1))
+            top = jnp.where(by, get(c, a, 3, 1), turn(get(c, a, 3, 0), -1))
+            low = jnp.where(by, turn(get(c, a, 0, 0), 1), get(c, a, 0, 1))
+            ye_ref[row, :] = jnp.where(ey, top, low)
+            yo_ref[row, :] = jnp.where(ey, low, top)
+            top = jnp.where(bx, get(c, 3, a, 1), turn(get(c, 3, a, 0), -2))
+            low = jnp.where(bx, turn(get(c, 0, a, 0), 2), get(c, 0, a, 1))
+            xe_ref[row, :] = jnp.where(ex, top, low)
+            xo_ref[row, :] = jnp.where(ex, low, top)
 
     total = jnp.zeros((8, 128), F32)
     sign = jnp.where(bk, 0.5, -0.5).astype(F32)
@@ -113,7 +124,7 @@
     at_wall = (bk & (lane == 127)) | (jnp.logical_not(bk) & (lane == 0))
     loads = jnp.sum(jnp.where(at_wall, total * sign, 0.0), axis=1, keepdims=True)
     part_ref[...] = jnp.zeros(part_ref.shape, F32)
-    lane1 = lax.broadcasted_iota(jnp.int32, (1, 128), 1)
+    lane1 = lax.broadcasted_iota(jnp.int32, (1, SN_DEV), 1)
     for side in range(2):
         for x in range(2):
             for y in range(2):
@@ -126,7 +137,7 @@
 
 
 def section_kernel(
-    s_ref, slot_ref, xl_ref, xh_ref, yl_ref, yh_ref, out_ref,
+    s_ref, slot_ref, ye_ref, yo_ref, xe_ref, xo_ref, out_ref,
     u_ref, f_ref, s3_ref, sm_ref, gx_ref, gy_ref, gz_ref,
 ):
     bx, by, bk = row_bit(2), row_bit(1), row_bit(4)
@@ -174,19 +185,22 @@
     def cell(src, c, i, j, h, off=0):
         return src[pl.ds(blk(c, i, j, h) + off, 8), :]
 
+    ex, ey = parity("group"), parity("dev")
     nodal(s_ref)
     for b in range(4):
         for h in range(2):
-            for d, g_ref, lo_ref, hi_ref, bit, step in (
-                (0, gx_ref, xl_ref, xh_ref, bx, 2),
-                (1, gy_ref, yl_ref, yh_ref, by, 1),
+            for d, g_ref, even_ref, odd_ref, even, bit, step in (
+                (0, gx_ref, xe_ref, xo_ref, ex, bx, 2),
+                (1, gy_ref, ye_ref, yo_ref, ey, by, 1),
             ):
                 first = (0, b) if d == 0 else (b, 0)
                 last = (3, b) if d == 0 else (b, 3)
                 uf = [cell(s_ref, c, *first, h) for c in range(5)]
                 ul = [cell(s_ref, c, *last, h) for c in range(5)]
-                hl = [lo_ref[pl.ds((c * 4 + b) * 8, 8), :] for c in range(5)]
-                hh = [hi_ref[pl.ds((c * 4 + b) * 8, 8), :] for c in range(5)]
+                he = [even_ref[pl.ds((c * 4 + b) * 8, 8), :] for c in range(5)]
+                ho = [odd_ref[pl.ds((c * 4 + b) * 8, 8), :] for c in range(5)]
+                hl = [jnp.where(even, ho[c], he[c]) for c in range(5)]
+                hh = [jnp.where(even, he[c], ho[c]) for c in range(5)]
                 if h == 1:
                     hl = [turn(t, -step) for t in hl]
                     hh = [turn(t, step) for t in hh]
@@ -335,24 +349,28 @@
     rows = state.reshape(ROWS, 128)
     halo = jax.ShapeDtypeStruct((160, 128), F32)
     vmem = pl.BlockSpec(memory_space=pltpu.VMEM)
-    xl, xh, yl, yh, part = pl.pallas_call(
+    ye, yo, xe, xo, part = pl.pallas_call(
         prepare_kernel,
-        out_shape=(halo, halo, halo, halo, jax.ShapeDtypeStruct((devices, 128), F32)),
+        out_shape=(halo, halo, halo, halo, jax.ShapeDtypeStruct((devices, SN_DEV), F32)),
         in_specs=[vmem, pl.BlockSpec(memory_space=pltpu.SMEM)],
         out_specs=(vmem,) * 5,
+        compiler_params=pltpu.CompilerParams(vmem_limit_bytes=VMEM_LIMIT),
         name="prepare",
         interpret=interpret,
     )(rows, wall_owner)
 
-    def shift(x, axis, by):
+    def swap(x, axis, odd):
         n = lax.axis_size(axis)
-        return lax.ppermute(x, axis, [(i, (i + by) % n) for i in range(n)])
-
-    xl, xh = shift(xl, "group", 1), shift(xh, "group", -1)
-    yl, yh = shift(yl, "dev", 1), shift(yh, "dev", -1)
+        edges = [(i, (i + 1) % n) for i in range(odd, n, 2)]
+        return lax.ppermute(x, axis, edges + [(b, a) for a, b in edges])
+
+    yo = swap(yo, "dev", 1)
+    xo = swap(xo, "group", 1)
+    ye = swap(ye, "dev", 0)
+    xe = swap(xe, "group", 0)
     parts = lax.all_to_all(part, ("group", "dev"), 0, 0, tiled=True)
-    wall_loads = jnp.sum(parts[:, :SN_DEV], axis=0)
-    out = pl.pallas_call(
+    wall_loads = jnp.sum(parts, axis=0)
+    section = pl.pallas_call(
         section_kernel,
         out_shape=jax.ShapeDtypeStruct((ROWS, 128), F32),
         in_specs=[vmem] * 6,
@@ -366,10 +384,12 @@
             pltpu.VMEM((640, 128), F32),
             pltpu.VMEM((640, 128), F32),
         ],
+        compiler_params=pltpu.CompilerParams(vmem_limit_bytes=VMEM_LIMIT),
         cost_estimate=pl.CostEstimate(flops=60_000_000, transcendentals=600_000, bytes_accessed=2_000_000),
         name="section",
         interpret=interpret,
-    )(rows, limit_slot.reshape(4, 128), xl, xh, yl, yh)
+    )
+    out = section(rows, limit_slot.reshape(4, 128), ye, yo, xe, xo)
     return out.reshape(state.shape), wall_loads
 
 

time: 39.9 us -> 42.8 us (1.073)
  the two profiles are of different devices: /device:TPU:120 before, /device:TPU:1 now
where the time goes in v2:
time: 42.8 us; the launch traced here: 42.6 us
  blocking collectives  19.4 us (45%)
  starting transfers between devices  11.7 us (27%)
  Pallas kernels  8.19 us (19%)
  local copies, waits for them, and re-layouts  1.77 us (4%)
  other arithmetic  0.8 us (2%)
  between operations  0.67 us (2%)
    all_to_all x1, blocking collectives, on_device(): parts = lax.all_to_all(part, ('group', 'dev'), 0, 0, tiled=True)  19.4 us
    ppermute x4, starting transfers between devices, swap(): return lax.ppermute(x, axis, edges + [(b, a) for a, b in edges])  11.7 us
    pallas_call x1, Pallas kernels, on_device(): out = section(rows, limit_slot.reshape(4, 128), ye, yo, xe, xo)  7.36 us
    unnamed x8, local copies, waits for them, and re-layouts  1.77 us
  transfers between devices with their start and end apart: 4, of which 0 were waited for; matrix products, arithmetic and copies ran while one was open for 2% of the time, Pallas kernels for 0%

profile of v2, /device:TPU:1, one launch (start us, length us, event | category | flops | bytes accessed | tf_op | source)
XLA Modules:
  0.0 42.6 jit_solution(17288302975039383999)
XLA Ops:
  0.6 0.0 copy-start
  0.6 1.1 %copy-done = f32[5,4,4,4,2,2,128]{6,5,4,3,2,1,0:T(2,128)S(1)} copy-done((f32[5,4,4,4,2,2,128]{6,5,4,3,2,1,0:T(2,128)S(1)}, f32[5,4,4,4,2,2,128]{6,5,4,3,2,1,0:T(2,128)}, u32[]{:S(2)}) %copy-start) | copy-done | bytes 655384
  1.7 0.0 copy-start.2
  1.7 0.7 %copy-done.2 = s32[2,2,2]{2,1,0:T(2,128)S(1)} copy-done((s32[2,2,2]{2,1,0:T(2,128)S(1)}, s32[2,2,2]{2,1,0:T(2,128)}, u32[]{:S(2)}) %copy-start.2) | copy-done | bytes 56
  2.4 0.0 copy-start.1
  2.4 0.8 %prepare.1 = (f32[160,128]{1,0:T(8,128)S(1)}, f32[160,128]{1,0:T(8,128)S(1)}, f32[160,128]{1,0:T(8,128)S(1)}, f32[160,128]{1,0:T(8,128)S(1)}, f32[256,8]{1,0:T(8,128)S(1)}) custom-call(f32[1280,128]{1,0:T(8,128)S(1)} %bitcast.6, s32[2,2,2]{2,1,0:T(2,128)S(1)} %copy-done.2), custom_call_target="tpu_custom_call" | custom-call | tf_op jit(solution)/shard_map/prepare/pallas_call | solution.py:352
  3.2 2.2 %collective-permute-start = (f32[160,128]{1,0:T(8,128)S(1)}, f32[160,128]{1,0:T(8,128)S(1)}, u32[]{:S(2)}, u32[]{:S(2)}) collective-permute-start(f32[160,128]{1,0:T(8,128)S(1)} %get-tuple-element.7), channel_id=1, source_target_pairs={{0,1},{2,3},{4,5},{6,7},{8,9},{10,11},{12,13},{14,15},{16,17},{18,... | collective-permute-start | bytes 245768 | tf_op jit(solution)/shard_map/ppermute | solution.py:365
  5.4 7.2 %collective-permute-start.1 = (f32[160,128]{1,0:T(8,128)S(1)}, f32[160,128]{1,0:T(8,128)S(1)}, u32[]{:S(2)}, u32[]{:S(2)}) collective-permute-start(f32[160,128]{1,0:T(8,128)S(1)} %get-tuple-element.8), channel_id=1, source_target_pairs={{1,2},{3,4},{5,6},{7,8},{9,10},{11,12},{13,14},{15,16},{17,18},{19... | collective-permute-start | bytes 245768 | tf_op jit(solution)/shard_map/ppermute | solution.py:365
  12.6 1.2 %collective-permute-start.2 = (f32[160,128]{1,0:T(8,128)S(1)}, f32[160,128]{1,0:T(8,128)S(1)}, u32[]{:S(2)}, u32[]{:S(2)}) collective-permute-start(f32[160,128]{1,0:T(8,128)S(1)} %get-tuple-element.9), channel_id=1, source_target_pairs={{0,32},{64,96},{128,160},{192,224},{32,0},{96,64},{160,128},{224,1... | collective-permute-start | bytes 245768 | tf_op jit(solution)/shard_map/ppermute | solution.py:365
  13.9 1.1 %collective-permute-start.3 = (f32[160,128]{1,0:T(8,128)S(1)}, f32[160,128]{1,0:T(8,128)S(1)}, u32[]{:S(2)}, u32[]{:S(2)}) collective-permute-start(f32[160,128]{1,0:T(8,128)S(1)} %get-tuple-element.10), channel_id=1, source_target_pairs={{32,64},{96,128},{160,192},{224,0},{64,32},{128,96},{192,160},{0,2... | collective-permute-start | bytes 245768 | tf_op jit(solution)/shard_map/ppermute | solution.py:365
  15.0 19.4 %all_to_all.9 = f32[256,1,8]{2,1,0:T(1,128)S(1)} all-to-all(f32[256,1,8]{2,1,0:T(1,128)S(1)} %bitcast.8), channel_id=1, replica_groups=mesh['group'=8,'dev'=32] {'group','dev'}, dimensions={0} | all-to-all | bytes 16384 | tf_op jit(solution)/shard_map/all_to_all | solution.py:371
  34.4 0.0 copy-start.3
  34.4 0.8 %reduce_sum.9 = f32[8]{0:T(128)} reduce(f32[256,1,8]{2,1,0:T(1,128)S(1)} %all_to_all.9, f32[]{:T(128)} %constant.0.clone.1), dimensions={0,1}, to_apply=%region_0.0 | reduce | flops 2040 | bytes 8228 | tf_op jit(solution)/shard_map/reduce_sum | solution.py:372
  35.2 0.0 collective-permute-done.ye_ref
  35.2 0.0 collective-permute-done.1.yo_ref
  35.2 0.0 collective-permute-done.2.xe_ref
  35.2 0.0 collective-permute-done.3.xo_ref
  35.2 0.0 copy-done.1
  35.2 0.0 copy-done.3
  35.2 7.4 %section.1 = f32[1280,128]{1,0:T(8,128)} custom-call(f32[1280,128]{1,0:T(8,128)S(1)} %bitcast.7, s32[4,128]{1,0:T(4,128)S(1)} %bitcast.9, f32[160,128]{1,0:T(8,128)S(1)} %collective-permute-done.ye_ref, f32[160,128]{1,0:T(8,128)S(1)} %collective-permute-done.1.yo_ref, f32[160,128]{1,0:T(8,128)S(1)} %collective-permute-done.2.xe_ref, ...), custom_call_target="tpu_custom_call" | custom-call | flops 60000000 | bytes 2000000 | tf_op jit(solution)/shard_map/section/pallas_call | solution.py:392
Async XLA Ops:
  0.6 1.1 %copy-start = (f32[5,4,4,4,2,2,128]{6,5,4,3,2,1,0:T(2,128)S(1)}, f32[5,4,4,4,2,2,128]{6,5,4,3,2,1,0:T(2,128)}, u32[]{:S(2)}) copy-start(f32[5,4,4,4,2,2,128]{6,5,4,3,2,1,0:T(2,128)} %param.3) | copy-start | bytes 1966084
  1.7 0.7 %copy-start.2 = (s32[2,2,2]{2,1,0:T(2,128)S(1)}, s32[2,2,2]{2,1,0:T(2,128)}, u32[]{:S(2)}) copy-start(s32[2,2,2]{2,1,0:T(2,128)} %own_ref.1) | copy-start | bytes 100
  2.4 32.8 %copy-start.1 = (f32[5,4,4,4,2,2,128]{6,5,4,3,2,1,0:T(2,128)S(1)}, f32[5,4,4,4,2,2,128]{6,5,4,3,2,1,0:T(2,128)}, u32[]{:S(2)}) copy-start(f32[5,4,4,4,2,2,128]{6,5,4,3,2,1,0:T(2,128)} %param.3) | copy-start | bytes 1966084
  3.2 32.0 %collective-permute-start = (f32[160,128]{1,0:T(8,128)S(1)}, f32[160,128]{1,0:T(8,128)S(1)}, u32[]{:S(2)}, u32[]{:S(2)}) collective-permute-start(f32[160,128]{1,0:T(8,128)S(1)} %get-tuple-element.7), channel_id=1, source_target_pairs={{0,1},{2,3},{4,5},{6,7},{8,9},{10,11},{12,13},{14,15},{16,17},{18,... | collective-permute-start | bytes 245768 | tf_op jit(solution)/shard_map/ppermute | solution.py:365
  5.4 29.8 %collective-permute-start.1 = (f32[160,128]{1,0:T(8,128)S(1)}, f32[160,128]{1,0:T(8,128)S(1)}, u32[]{:S(2)}, u32[]{:S(2)}) collective-permute-start(f32[160,128]{1,0:T(8,128)S(1)} %get-tuple-element.8), channel_id=1, source_target_pairs={{1,2},{3,4},{5,6},{7,8},{9,10},{11,12},{13,14},{15,16},{17,18},{19... | collective-permute-start | bytes 245768 | tf_op jit(solution)/shard_map/ppermute | solution.py:365
  12.6 22.6 %collective-permute-start.2 = (f32[160,128]{1,0:T(8,128)S(1)}, f32[160,128]{1,0:T(8,128)S(1)}, u32[]{:S(2)}, u32[]{:S(2)}) collective-permute-start(f32[160,128]{1,0:T(8,128)S(1)} %get-tuple-element.9), channel_id=1, source_target_pairs={{0,32},{64,96},{128,160},{192,224},{32,0},{96,64},{160,128},{224,1... | collective-permute-start | bytes 245768 | tf_op jit(solution)/shard_map/ppermute | solution.py:365
  13.9 21.3 %collective-permute-start.3 = (f32[160,128]{1,0:T(8,128)S(1)}, f32[160,128]{1,0:T(8,128)S(1)}, u32[]{:S(2)}, u32[]{:S(2)}) collective-permute-start(f32[160,128]{1,0:T(8,128)S(1)} %get-tuple-element.10), channel_id=1, source_target_pairs={{32,64},{96,128},{160,192},{224,0},{64,32},{128,96},{192,160},{0,2... | collective-permute-start | bytes 245768 | tf_op jit(solution)/shard_map/ppermute | solution.py:365
  34.4 0.8 %copy-start.3 = (s32[2,2,128]{2,1,0:T(2,128)S(1)}, s32[2,2,128]{2,1,0:T(2,128)}, u32[]{:S(2)}) copy-start(s32[2,2,128]{2,1,0:T(2,128)} %param.4) | copy-start | bytes 6148

commit v3 on v2

v3 whole, which is shorter than its diff:
```python
import jax
import jax.numpy as jnp
import numpy as np
from jax import lax
from jax.experimental import pallas as pl
from jax.experimental.pallas import tpu as pltpu
from jax.sharding import PartitionSpec as P


SUBSTEPS = 8
SN_DEV = 8
GAMMA = 1.4
COURANT = 0.02
F32 = jnp.float32

ROWS = 1280
VMEM_LIMIT = 16 * 1024 * 1024


def blk(v, i, j, h):
    return (((v * 4 + i) * 4 + j) * 2 + h) * 8


def nod(q, i, j, h):
    return q * 256 + ((i * 4 + j) * 2 + h) * 8


FLUX_OF = (
    (None, 0, 1, 2, 6),
    (None, 1, 3, 4, 7),
    (None, 2, 4, 5, 8),
)


def derivative_table():
    gll_nodes = np.array([-1.0, -np.sqrt(0.2), np.sqrt(0.2), 1.0])
    bary = np.array(
        [1.0 / np.prod([gll_nodes[a] - gll_nodes[b] for b in range(4) if b != a]) for a in range(4)]
    )
    table = np.zeros((4, 4))
    for a in range(4):
        for b in range(4):
            if a != b:
                table[a, b] = bary[b] / bary[a] / (gll_nodes[a] - gll_nodes[b])
    for a in (0, 3):
        table[a, a] = -np.sum(table[a])
    return table


WEIGHTS = np.array([1.0, 5.0, 5.0, 1.0]) / 6.0


def row_bit(bit):
    rows = lax.broadcasted_iota(jnp.int32, (8, 128), 0)
    return (rows & bit) != 0


def turn(x, shift):
    return pltpu.roll(x, shift % 8, 0)


def root(x):
    return x * lax.rsqrt(jnp.maximum(x, 1e-30))


def point_flux(u, d):
    inv = 1.0 / u[0]
    v = u[1 + d] * inv
    ke = (u[1] * u[1] + u[2] * u[2] + u[3] * u[3]) * inv
    p = (GAMMA - 1.0) * (u[4] - 0.5 * ke)
    flux = [u[1 + d]] + [u[1 + a] * v for a in range(3)] + [v * (u[4] + p)]
    flux[1 + d] = flux[1 + d] + p
    speed = jnp.abs(v) + root(GAMMA * p * inv)
    return flux, speed


def twice_face(fl, fr, s, ul, ur):
    return (fl + fr) - s * (ur - ul)


def z_wall_pair(own, lane):
    low = jnp.logical_not(row_bit(4))
    wall = (low & (lane == 0)) | (row_bit(4) & (lane == 127))
    across = []
    for c in range(5):
        x = turn(own[c], 4)
        n = jnp.where(low, pltpu.roll(x, 1, 1), pltpu.roll(x, 127, 1))
        across.append(jnp.where(wall, -own[c] if c == 3 else own[c], n))
    return across


def parity(axis):
    return jnp.full((8, 128), lax.axis_index(axis) % 2, jnp.int32) == 0


def prepare_kernel(
    state_ref, owner_ref, ye_ref, yo_ref, xe_ref, xo_ref, part_out_ref, s_ref, own_ref, part_ref, sems
):
    fetch = pltpu.make_async_copy(state_ref, s_ref, sems.at[0])
    fetch_own = pltpu.make_async_copy(owner_ref, own_ref, sems.at[1])
    store_part = pltpu.make_async_copy(part_ref, part_out_ref, sems.at[2])
    fetch.start()
    fetch_own.start()
    part_ref[...] = jnp.zeros(part_ref.shape, F32)
    bx, by, bk = row_bit(2), row_bit(1), row_bit(4)
    lane = lax.broadcasted_iota(jnp.int32, (8, 128), 1)
    ex, ey = parity("group"), parity("dev")
    fetch.wait()
    fetch_own.wait()

    def get(v, i, j, h):
        return s_ref[pl.ds(blk(v, i, j, h), 8), :]

    total = jnp.zeros((8, 128), F32)
    sign = jnp.where(bk, 0.5, -0.5).astype(F32)
    for i in range(4):
        for j in range(4):
            own = [jnp.where(bk, get(c, i, j, 1), get(c, i, j, 0)) for c in range(5)]
            across = list(own)
            across[3] = -own[3]
            fo, so = point_flux(own, 2)
            fa, sa = point_flux(across, 2)
            jump = jnp.where(bk, across[3] - own[3], own[3] - across[3])
            flux = (fo[3] + fa[3]) - jnp.maximum(so, sa) * jump
            total = total + float(WEIGHTS[i] * WEIGHTS[j]) * flux
    at_wall = (bk & (lane == 127)) | (jnp.logical_not(bk) & (lane == 0))
    loads = jnp.sum(jnp.where(at_wall, total * sign, 0.0), axis=1, keepdims=True)
    lane1 = lax.broadcasted_iota(jnp.int32, (1, SN_DEV), 1)
    for side in range(2):
        for x in range(2):
            for y in range(2):
                node = own_ref[x, y, side]
                r = side * 4 + x * 2 + y
                at = pl.ds(node // SN_DEV, 1)
                part_ref[at, :] = part_ref[at, :] + jnp.where(
                    lane1 == node % SN_DEV, loads[r : r + 1, :], 0.0
                )
    store_part.start()
    for c in range(5):
        for a in range(4):
            row = pl.ds((c * 4 + a) * 8, 8)
            top = jnp.where(by, get(c, a, 3, 1), turn(get(c, a, 3, 0), -1))
            low = jnp.where(by, turn(get(c, a, 0, 0), 1), get(c, a, 0, 1))
            ye_ref[row, :] = jnp.where(ey, top, low)
            yo_ref[row, :] = jnp.where(ey, low, top)
            top = jnp.where(bx, get(c, 3, a, 1), turn(get(c, 3, a, 0), -2))
            low = jnp.where(bx, turn(get(c, 0, a, 0), 2), get(c, 0, a, 1))
            xe_ref[row, :] = jnp.where(ex, top, low)
            xo_ref[row, :] = jnp.where(ex, low, top)
    store_part.wait()


def sum_kernel(parts_ref, loads_ref):
    loads_ref[...] = jnp.sum(parts_ref[...], axis=0, keepdims=True)


IJ = [(i, j) for i in range(4) for j in range(4)]


def cell(src, c, i, j, h, off=0):
    return src[pl.ds(blk(c, i, j, h) + off, 8), :]


def flux_of(src, f_ref, d, c, i, j, h, off=0):
    if c == 0:
        return cell(src, 1 + d, i, j, h, off)
    return f_ref[pl.ds(nod(FLUX_OF[d][c], i, j, h) + off, 8), :]


def face_at(g_ref, side, c, b, h):
    return g_ref[pl.ds(side * 320 + ((c * 4 + b) * 2 + h) * 8, 8), :]


def z_face_at(gz_ref, c, i, j):
    return gz_ref[pl.ds(((c * 4 + i) * 4 + j) * 8, 8), :]


def nodal(src, f_ref, s3_ref=None, sm_ref=None):
    for i, j in IJ:
        for h in range(2):
            u = [cell(src, c, i, j, h) for c in range(5)]
            inv = 1.0 / u[0]
            v = [u[1 + d] * inv for d in range(3)]
            xx, xy, xz = u[1] * v[0], u[1] * v[1], u[1] * v[2]
            yy, yz, zz = u[2] * v[1], u[2] * v[2], u[3] * v[2]
            p = (GAMMA - 1.0) * (u[4] - 0.5 * (xx + yy + zz))
            e = u[4] + p
            q = [xx + p, xy, xz, yy + p, yz, zz + p, v[0] * e, v[1] * e, v[2] * e]
            for n in range(9):
                f_ref[pl.ds(nod(n, i, j, h), 8), :] = q[n]
            if s3_ref is not None:
                sound = root(GAMMA * p * inv)
                for d in range(3):
                    s3_ref[pl.ds(nod(d, i, j, h), 8), :] = jnp.abs(v[d]) + sound
    if s3_ref is None:
        return

    def speed(d, i, j, h, off=0):
        return s3_ref[pl.ds(nod(d, i, j, h) + off, 8), :]

    for a in range(3):
        for b in range(4):
            for h in range(2):
                sm_ref[pl.ds(nod(0, a, b, h), 8), :] = jnp.maximum(
                    speed(0, a, b, h), speed(0, a + 1, b, h)
                )
                sm_ref[pl.ds(nod(1, b, a, h), 8), :] = jnp.maximum(
                    speed(1, b, a, h), speed(1, b, a + 1, h)
                )
    for i, j in IJ:
        mid = speed(2, i, j, 0, 4)
        for h in range(2):
            sm_ref[pl.ds(nod(2, i, j, h), 8), :] = jnp.maximum(speed(2, i, j, h), mid)


def pair(lo_value, hi_value):
    return jnp.where(row_bit(4), float(hi_value), float(lo_value)).astype(F32)


LIFT = COURANT * 0.5 / WEIGHTS[0]


def volume_kernel(s_ref, gz_ref, dg_ref, f_ref):
    bk = row_bit(4)
    lane = lax.broadcasted_iota(jnp.int32, (8, 128), 1)
    nodal(s_ref, f_ref)
    for i, j in IJ:
        own = [jnp.where(bk, cell(s_ref, c, i, j, 1), cell(s_ref, c, i, j, 0)) for c in range(5)]
        across = z_wall_pair(own, lane)
        fo, so = point_flux(own, 2)
        fa, sa = point_flux(across, 2)
        s = jnp.maximum(so, sa)
        s = jnp.where(bk, s, -s)
        for c in range(5):
            gz_ref[pl.ds(((c * 4 + i) * 4 + j) * 8, 8), :] = (fo[c] + fa[c]) - s * (across[c] - own[c])

    table = derivative_table()
    table[0, 0] += 1.0 / WEIGHTS[0]
    table[3, 3] -= 1.0 / WEIGHTS[3]
    table = COURANT * table
    zc = [
        [pair(table[2 * h, 2 * g], table[2 * h + 1, 2 * g + 1]) for g in range(2)]
        + [pair(table[2 * h, 2 * g + 1], table[2 * h + 1, 2 * g]) for g in range(2)]
        for h in range(2)
    ]
    zl = [pair(-LIFT, 0.0), pair(0.0, LIFT)]
    for c in range(5):
        for h in range(2):
            acc = {}
            for b in range(4):
                for d in range(2):
                    line = [(a, b) if d == 0 else (b, a) for a in range(4)]
                    fl = [flux_of(s_ref, f_ref, d, c, *n, h) for n in line]
                    for a in range(4):
                        terms = [float(table[a, m]) * fl[m] for m in range(4) if table[a, m] != 0.0]
                        acc.setdefault(line[a], []).append(sum(terms[1:], terms[0]))
            for i, j in IJ:
                fa = flux_of(s_ref, f_ref, 2, c, i, j, 0)
                fb = flux_of(s_ref, f_ref, 2, c, i, j, 1)
                r = zc[h][0] * fa + zc[h][1] * fb + zc[h][2] * turn(fa, 4) + zc[h][3] * turn(fb, 4)
                r = r + zl[h] * z_face_at(gz_ref, c, i, j)
                r = r + (acc[i, j][0] + acc[i, j][1])
                dg_ref[pl.ds(blk(c, i, j, h), 8), :] = cell(s_ref, c, i, j, h) - r


def section_kernel(
    s_ref, slots_ref, ye_ref, yo_ref, xe_ref, xo_ref, gz_ref, dg_ref, result_ref,
    u_ref, f_ref, s3_ref, sm_ref, gx_ref, gy_ref, out_ref, slot_ref, sems,
):
    fetch_slot = pltpu.make_async_copy(slots_ref, slot_ref, sems.at[5])
    fetch_slot.start()
    bx, by, bk = row_bit(2), row_bit(1), row_bit(4)
    low = jnp.logical_not(bk)
    ex, ey = parity("group"), parity("dev")
    nodal(s_ref, f_ref, s3_ref, sm_ref)
    for b in range(4):
        for h in range(2):
            for d, g_ref, even_ref, odd_ref, even, bit, step in (
                (0, gx_ref, xe_ref, xo_ref, ex, bx, 2),
                (1, gy_ref, ye_ref, yo_ref, ey, by, 1),
            ):
                first = (0, b) if d == 0 else (b, 0)
                last = (3, b) if d == 0 else (b, 3)
                uf = [cell(s_ref, c, *first, h) for c in range(5)]
                ul = [cell(s_ref, c, *last, h) for c in range(5)]
                he = [even_ref[pl.ds((c * 4 + b) * 8, 8), :] for c in range(5)]
                ho = [odd_ref[pl.ds((c * 4 + b) * 8, 8), :] for c in range(5)]
                hl = [jnp.where(even, ho[c], he[c]) for c in range(5)]
                hh = [jnp.where(even, he[c], ho[c]) for c in range(5)]
                if h == 1:
                    hl = [turn(t, -step) for t in hl]
                    hh = [turn(t, step) for t in hh]
                before = [jnp.where(bit, turn(ul[c], step), hl[c]) for c in range(5)]
                after = [jnp.where(bit, hh[c], turn(uf[c], -step)) for c in range(5)]
                fb, sb = point_flux(before, d)
                fa, sa = point_flux(after, d)
                sl = jnp.maximum(sb, s3_ref[pl.ds(nod(d, *first, h), 8), :])
                sh = jnp.maximum(sa, s3_ref[pl.ds(nod(d, *last, h), 8), :])
                for c in range(5):
                    at = ((c * 4 + b) * 2 + h) * 8
                    g_ref[pl.ds(at, 8), :] = twice_face(
                        fb[c], flux_of(s_ref, f_ref, d, c, *first, h), sl, before[c], uf[c]
                    )
                    g_ref[pl.ds(320 + at, 8), :] = twice_face(
                        flux_of(s_ref, f_ref, d, c, *last, h), fa[c], sh, ul[c], after[c]
                    )

    scale = COURANT / SUBSTEPS * 0.5 / WEIGHTS
    kz = [pair(scale[0], scale[1]), pair(scale[2], scale[3])]

    def advance(src, put, finish):
        for c in range(5):
            done = {}
            for h in range(2):
                diff = {}
                for b in range(4):
                    for d in range(2):
                        line = [(a, b) if d == 0 else (b, a) for a in range(4)]
                        g_ref = gx_ref if d == 0 else gy_ref
                        u = [cell(src, c, *n, h) for n in line]
                        f = [flux_of(src, f_ref, d, c, *n, h) for n in line]
                        g = [face_at(g_ref, 0, c, b, h)]
                        for a in range(3):
                            s = sm_ref[pl.ds(nod(d, *line[a], h), 8), :]
                            g.append(twice_face(f[a], f[a + 1], s, u[a], u[a + 1]))
                        g.append(face_at(g_ref, 1, c, b, h))
                        for a in range(4):
                            diff[d, line[a]] = g[a + 1] - g[a]
                for i, j in IJ:
                    if scale[i] == scale[j]:
                        r = float(scale[i]) * (diff[0, (i, j)] + diff[1, (i, j)])
                    else:
                        r = float(scale[i]) * diff[0, (i, j)] + float(scale[j]) * diff[1, (i, j)]
                    u = cell(src, c, i, j, h)
                    um = cell(src, c, i, j, 0, 4)
                    fz = flux_of(src, f_ref, 2, c, i, j, h)
                    fm = flux_of(src, f_ref, 2, c, i, j, 0, 4)
                    s = sm_ref[pl.ds(nod(2, i, j, h), 8), :]
                    gz = z_face_at(gz_ref, c, i, j)
                    if h == 0:
                        t = twice_face(fz, fm, s, u, um)
                        dz = t - jnp.where(low, gz, turn(t, 4))
                    else:
                        t = twice_face(fm, fz, s, um, u)
                        dz = jnp.where(low, turn(t, 4), gz) - t
                    done[i, j, h] = u - (r + kz[h] * dz)
            for (i, j, h), value in done.items():
                put(c, i, j, h, value)
            finish(c)

    def put_u(c, i, j, h, value):
        u_ref[pl.ds(blk(c, i, j, h), 8), :] = value

    def put_out(c, i, j, h, value):
        at = pl.ds(blk(c, i, j, h), 8)
        dg = dg_ref[at, :]
        for n, b, g_ref in ((i, j, gx_ref), (j, i, gy_ref)):
            if n == 0:
                dg = dg + float(LIFT) * face_at(g_ref, 0, c, b, h)
            if n == 3:
                dg = dg - float(LIFT) * face_at(g_ref, 1, c, b, h)
        out_ref[at, :] = jnp.where(troubled, value, dg)

    def store(c):
        rows = pl.ds(c * 256, 256)
        return pltpu.make_async_copy(out_ref.at[rows, :], result_ref.at[rows, :], sems.at[c])

    u_ref[...] = s_ref[...]

    def substep(_, carry):
        advance(u_ref, put_u, lambda c: None)
        nodal(u_ref, f_ref, s3_ref, sm_ref)
        return carry

    lax.fori_loop(0, SUBSTEPS - 1, substep, 0)
    fetch_slot.wait()
    slot = slot_ref[...]
    troubled = jnp.concatenate([slot, slot], axis=0) >= 0
    advance(u_ref, put_out, lambda c: store(c).start())
    for c in range(5):
        store(c).wait()


def on_device(state, limit_slot, wall_owner, interpret=False):
    n_group, n_dev = lax.axis_size("group"), lax.axis_size("dev")
    devices = n_group * n_dev
    rows = state.reshape(ROWS, 128)
    halo = jax.ShapeDtypeStruct((160, 128), F32)
    vmem = pl.BlockSpec(memory_space=pltpu.VMEM)
    hbm = pl.BlockSpec(memory_space=pltpu.HBM)
    ye, yo, xe, xo, part = pl.pallas_call(
        prepare_kernel,
        out_shape=(halo, halo, halo, halo, jax.ShapeDtypeStruct((devices, SN_DEV), F32)),
        in_specs=[hbm, hbm],
        out_specs=(vmem,) * 4 + (hbm,),
        scratch_shapes=[
            pltpu.VMEM((ROWS, 128), F32),
            pltpu.SMEM((2, 2, 2), jnp.int32),
            pltpu.VMEM((devices, SN_DEV), F32),
            pltpu.SemaphoreType.DMA((3,)),
        ],
        compiler_params=pltpu.CompilerParams(vmem_limit_bytes=VMEM_LIMIT),
        name="prepare",
        interpret=interpret,
    )(
        pltpu.with_memory_space_constraint(rows, pltpu.HBM),
        pltpu.with_memory_space_constraint(wall_owner, pltpu.HBM),
    )

    def swap(x, axis, odd):
        n = lax.axis_size(axis)
        edges = [(i, (i + 1) % n) for i in range(odd, n, 2)]
        return lax.ppermute(x, axis, edges + [(b, a) for a, b in edges])

    yo = swap(yo, "dev", 1)
    xo = swap(xo, "group", 1)
    ye = swap(ye, "dev", 0)
    xe = swap(xe, "group", 0)
    parts = lax.all_to_all(part, ("group", "dev"), 0, 0, tiled=True)
    wall_loads = pl.pallas_call(
        sum_kernel,
        out_shape=jax.ShapeDtypeStruct((1, SN_DEV), F32),
        in_specs=[vmem],
        out_specs=vmem,
        compiler_params=pltpu.CompilerParams(vmem_limit_bytes=VMEM_LIMIT),
        name="wall_sum",
        interpret=interpret,
    )(parts).reshape(SN_DEV)
    small = pltpu.CompilerParams(vmem_limit_bytes=VMEM_LIMIT)
    volume = pl.pallas_call(
        volume_kernel,
        out_shape=(jax.ShapeDtypeStruct((640, 128), F32), jax.ShapeDtypeStruct((ROWS, 128), F32)),
        in_specs=[vmem],
        out_specs=(vmem, vmem),
        scratch_shapes=[pltpu.VMEM((9 * 256, 128), F32)],
        compiler_params=small,
        name="volume",
        interpret=interpret,
    )
    section = pl.pallas_call(
        section_kernel,
        out_shape=jax.ShapeDtypeStruct((ROWS, 128), F32),
        in_specs=[vmem, hbm] + [vmem] * 6,
        out_specs=hbm,
        scratch_shapes=[
            pltpu.VMEM((ROWS, 128), F32),
            pltpu.VMEM((9 * 256, 128), F32),
            pltpu.VMEM((3 * 256, 128), F32),
            pltpu.VMEM((3 * 256, 128), F32),
            pltpu.VMEM((640, 128), F32),
            pltpu.VMEM((640, 128), F32),
            pltpu.VMEM((ROWS, 128), F32),
            pltpu.VMEM((4, 128), jnp.int32),
            pltpu.SemaphoreType.DMA((6,)),
        ],
        compiler_params=small,
        cost_estimate=pl.CostEstimate(flops=60_000_000, transcendentals=600_000, bytes_accessed=2_000_000),
        name="section",
        interpret=interpret,
    )
    gz, dg = volume(rows)
    slots = pltpu.with_memory_space_constraint(limit_slot.reshape(4, 128), pltpu.HBM)
    out = section(rows, slots, ye, yo, xe, xo, gz, dg)
    return out.reshape(state.shape), wall_loads


def solution(mesh):
    in_specs = (
        P(None, None, None, None, "group", "dev", None),
        P("group", "dev", None),
        P("group", "dev", None),
    )
    out_specs = (P(None, None, None, None, "group", "dev", None), P(("group", "dev")))
    return jax.shard_map(
        on_device, mesh=mesh, in_specs=in_specs, out_specs=out_specs, check_vma=False
    )
```

time: 42.8 us -> 41 us (0.958)
  blocking collectives: 19.4 us -> 0 us
  waiting for transfers between devices: 0.01 us -> 11.7 us
  starting transfers between devices: 11.7 us -> 18.7 us
  local copies, waits for them, and re-layouts: 1.77 us -> 0.01 us
  Pallas kernels: 8.19 us -> 9.82 us
  other arithmetic: 0.8 us -> 0 us
    all_to_all x1 -> x0, blocking collectives: 19.4 us -> none  [on_device(): parts = lax.all_to_all(part, ('group', 'dev'), 0, 0, tiled=True)]
    all_to_all x0 -> x1, waiting for transfers between devices: none -> 11.7 us  [on_device(): parts = lax.all_to_all(part, ('group', 'dev'), 0, 0, tiled=True)]
    all_to_all x0 -> x1, starting transfers between devices: none -> 7 us  [on_device(): parts = lax.all_to_all(part, ('group', 'dev'), 0, 0, tiled=True)]
    unnamed x8 -> x2, local copies, waits for them, and re-layouts: 1.77 us -> 0.01 us
    pallas_call x1, Pallas kernels: 0.83 us -> 2.05 us  [on_device(): pl.pallas_call(prepare_kernel, out_shape=(halo, halo, halo, halo, jax.Sha...]
    reduce_sum x1 -> x0, other arithmetic: 0.8 us -> none  [on_device(): wall_loads = jnp.sum(parts, axis=0)]
    pallas_call x1 -> x3, Pallas kernels: 7.36 us -> 7.77 us  [the longest x1 6.33 us: on_device(): out = section(rows, slots, ye, yo, xe, xo, gz, dg)]
  transfers between devices with their start and end apart: 4 -> 5, of which waited for: 0 -> 1; matrix products, arithmetic and copies ran while one was open for 2% -> 0% of each run, Pallas kernels for 0% -> 4%
where the time goes in v3:
time: 41 us; the launch traced here: 40.9 us
  starting transfers between devices  18.7 us (46%)
  waiting for transfers between devices  11.7 us (29%)
  Pallas kernels  9.82 us (24%)
  between operations  0.68 us (2%)
    ppermute x4, starting transfers between devices, swap(): return lax.ppermute(x, axis, edges + [(b, a) for a, b in edges])  11.7 us
    all_to_all x1, waiting for transfers between devices, on_device(): parts = lax.all_to_all(part, ('group', 'dev'), 0, 0, tiled=True)  11.7 us
    all_to_all x1, starting transfers between devices, on_device(): parts = lax.all_to_all(part, ('group', 'dev'), 0, 0, tiled=True)  7 us
    pallas_call x1, Pallas kernels, on_device(): out = section(rows, slots, ye, yo, xe, xo, gz, dg)  6.33 us
    pallas_call x1, Pallas kernels, on_device(): pl.pallas_call(prepare_kernel, out_shape=(halo, halo, halo, halo, jax.Sha...  2.05 us
    pallas_call x1, Pallas kernels, on_device(): gz, dg = volume(rows)  0.89 us
  transfers between devices with their start and end apart: 5, of which 1 were waited for; matrix products, arithmetic and copies ran while one was open for 0% of the time, Pallas kernels for 4%

profile of v3, /device:TPU:1, one launch (start us, length us, event | category | flops | bytes accessed | tf_op | source)
XLA Modules:
  0.0 40.9 jit_solution(9298366668500993955)
XLA Ops:
  0.6 0.0 copy-start
  0.6 2.1 %prepare.1 = (f32[160,128]{1,0:T(8,128)S(1)}, f32[160,128]{1,0:T(8,128)S(1)}, f32[160,128]{1,0:T(8,128)S(1)}, f32[160,128]{1,0:T(8,128)S(1)}, f32[256,8]{1,0:T(8,128)}) custom-call(f32[1280,128]{1,0:T(8,128)} %bitcast.8, s32[2,2,2]{2,1,0:T(2,128)} %owner_ref.1), custom_call_target="tpu_custom_call" | custom-call | tf_op jit(solution)/shard_map/prepare/pallas_call | solution.py:391
  2.7 2.2 %collective-permute-start = (f32[160,128]{1,0:T(8,128)S(1)}, f32[160,128]{1,0:T(8,128)S(1)}, u32[]{:S(2)}, u32[]{:S(2)}) collective-permute-start(f32[160,128]{1,0:T(8,128)S(1)} %get-tuple-element.9), channel_id=1, source_target_pairs={{0,1},{2,3},{4,5},{6,7},{8,9},{10,11},{12,13},{14,15},{16,17},{18,... | collective-permute-start | bytes 245768 | tf_op jit(solution)/shard_map/ppermute | solution.py:413
  4.9 7.2 %collective-permute-start.1 = (f32[160,128]{1,0:T(8,128)S(1)}, f32[160,128]{1,0:T(8,128)S(1)}, u32[]{:S(2)}, u32[]{:S(2)}) collective-permute-start(f32[160,128]{1,0:T(8,128)S(1)} %get-tuple-element.10), channel_id=1, source_target_pairs={{1,2},{3,4},{5,6},{7,8},{9,10},{11,12},{13,14},{15,16},{17,18},{19... | collective-permute-start | bytes 245768 | tf_op jit(solution)/shard_map/ppermute | solution.py:413
  12.1 1.2 %collective-permute-start.2 = (f32[160,128]{1,0:T(8,128)S(1)}, f32[160,128]{1,0:T(8,128)S(1)}, u32[]{:S(2)}, u32[]{:S(2)}) collective-permute-start(f32[160,128]{1,0:T(8,128)S(1)} %get-tuple-element.11), channel_id=1, source_target_pairs={{0,32},{64,96},{128,160},{192,224},{32,0},{96,64},{160,128},{224,1... | collective-permute-start | bytes 245768 | tf_op jit(solution)/shard_map/ppermute | solution.py:413
  13.3 1.1 %collective-permute-start.3 = (f32[160,128]{1,0:T(8,128)S(1)}, f32[160,128]{1,0:T(8,128)S(1)}, u32[]{:S(2)}, u32[]{:S(2)}) collective-permute-start(f32[160,128]{1,0:T(8,128)S(1)} %get-tuple-element.12), channel_id=1, source_target_pairs={{32,64},{96,128},{160,192},{224,0},{64,32},{128,96},{192,160},{0,2... | collective-permute-start | bytes 245768 | tf_op jit(solution)/shard_map/ppermute | solution.py:413
  14.4 7.0 %all-to-all-start = ((f32[256,1,8]{2,1,0:T(1,128)}), f32[256,1,8]{2,1,0:T(1,128)S(1)}, u32[]{:S(2)}, u32[]{:S(2)}) async-start(f32[256,1,8]{2,1,0:T(1,128)} %bitcast.4), calls=%async_computation | async-start | bytes 262144 | tf_op jit(solution)/shard_map/all_to_all | solution.py:419
  21.4 0.0 copy-done
  21.4 0.9 %volume.1 = (f32[640,128]{1,0:T(8,128)S(1)}, f32[1280,128]{1,0:T(8,128)S(1)}) custom-call(f32[1280,128]{1,0:T(8,128)S(1)} %bitcast.9), custom_call_target="tpu_custom_call" | custom-call | tf_op jit(solution)/shard_map/volume/pallas_call | solution.py:461
  22.3 11.7 %all-to-all-done = f32[256,1,8]{2,1,0:T(1,128)S(1)} async-done(((f32[256,1,8]{2,1,0:T(1,128)}), f32[256,1,8]{2,1,0:T(1,128)S(1)}, u32[]{:S(2)}, u32[]{:S(2)}) %all-to-all-start) | async-done | bytes 8224 | tf_op jit(solution)/shard_map/all_to_all | solution.py:419
  34.0 0.6 %wall_sum.1 = f32[1,8]{1,0:T(1,128)} custom-call(f32[256,8]{1,0:T(8,128)S(1)} %bitcast.11), custom_call_target="tpu_custom_call" | custom-call | tf_op jit(solution)/shard_map/wall_sum/pallas_call | solution.py:420
  34.5 0.0 collective-permute-done.ye_ref
  34.5 0.0 collective-permute-done.1.yo_ref
  34.6 0.0 collective-permute-done.2.xe_ref
  34.6 0.0 collective-permute-done.3.xo_ref
  34.6 6.3 %section.1 = f32[1280,128]{1,0:T(8,128)} custom-call(f32[1280,128]{1,0:T(8,128)S(1)} %bitcast.10, s32[4,128]{1,0:T(4,128)} %bitcast.13, f32[160,128]{1,0:T(8,128)S(1)} %collective-permute-done.ye_ref, f32[160,128]{1,0:T(8,128)S(1)} %collective-permute-done.1.yo_ref, f32[160,128]{1,0:T(8,128)S(1)} %collective-permute-done.2.xe_ref, ...), custom_call_target="tpu_custom_call" | custom-call | flops 60000000 | bytes 2000000 | tf_op jit(solution)/shard_map/section/pallas_call | solution.py:463
Async XLA Ops:
  0.6 20.8 %copy-start = (f32[5,4,4,4,2,2,128]{6,5,4,3,2,1,0:T(2,128)S(1)}, f32[5,4,4,4,2,2,128]{6,5,4,3,2,1,0:T(2,128)}, u32[]{:S(2)}) copy-start(f32[5,4,4,4,2,2,128]{6,5,4,3,2,1,0:T(2,128)} %param.3) | copy-start | bytes 1966084
  2.7 31.8 %collective-permute-start = (f32[160,128]{1,0:T(8,128)S(1)}, f32[160,128]{1,0:T(8,128)S(1)}, u32[]{:S(2)}, u32[]{:S(2)}) collective-permute-start(f32[160,128]{1,0:T(8,128)S(1)} %get-tuple-element.9), channel_id=1, source_target_pairs={{0,1},{2,3},{4,5},{6,7},{8,9},{10,11},{12,13},{14,15},{16,17},{18,... | collective-permute-start | bytes 245768 | tf_op jit(solution)/shard_map/ppermute | solution.py:413
  4.9 29.7 %collective-permute-start.1 = (f32[160,128]{1,0:T(8,128)S(1)}, f32[160,128]{1,0:T(8,128)S(1)}, u32[]{:S(2)}, u32[]{:S(2)}) collective-permute-start(f32[160,128]{1,0:T(8,128)S(1)} %get-tuple-element.10), channel_id=1, source_target_pairs={{1,2},{3,4},{5,6},{7,8},{9,10},{11,12},{13,14},{15,16},{17,18},{19... | collective-permute-start | bytes 245768 | tf_op jit(solution)/shard_map/ppermute | solution.py:413
  12.1 22.5 %collective-permute-start.2 = (f32[160,128]{1,0:T(8,128)S(1)}, f32[160,128]{1,0:T(8,128)S(1)}, u32[]{:S(2)}, u32[]{:S(2)}) collective-permute-start(f32[160,128]{1,0:T(8,128)S(1)} %get-tuple-element.11), channel_id=1, source_target_pairs={{0,32},{64,96},{128,160},{192,224},{32,0},{96,64},{160,128},{224,1... | collective-permute-start | bytes 245768 | tf_op jit(solution)/shard_map/ppermute | solution.py:413
  13.3 21.2 %collective-permute-start.3 = (f32[160,128]{1,0:T(8,128)S(1)}, f32[160,128]{1,0:T(8,128)S(1)}, u32[]{:S(2)}, u32[]{:S(2)}) collective-permute-start(f32[160,128]{1,0:T(8,128)S(1)} %get-tuple-element.12), channel_id=1, source_target_pairs={{32,64},{96,128},{160,192},{224,0},{64,32},{128,96},{192,160},{0,2... | collective-permute-start | bytes 245768 | tf_op jit(solution)/shard_map/ppermute | solution.py:413
  14.4 19.6 %all-to-all-start = ((f32[256,1,8]{2,1,0:T(1,128)}), f32[256,1,8]{2,1,0:T(1,128)S(1)}, u32[]{:S(2)}, u32[]{:S(2)}) async-start(f32[256,1,8]{2,1,0:T(1,128)} %bitcast.4), calls=%async_computation | async-start | bytes 262144 | tf_op jit(solution)/shard_map/all_to_all | solution.py:419

commit v4 on v3

--- a/solution.py
+++ b/solution.py
@@ -116,12 +116,8 @@
     for i in range(4):
         for j in range(4):
             own = [jnp.where(bk, get(c, i, j, 1), get(c, i, j, 0)) for c in range(5)]
-            across = list(own)
-            across[3] = -own[3]
             fo, so = point_flux(own, 2)
-            fa, sa = point_flux(across, 2)
-            jump = jnp.where(bk, across[3] - own[3], own[3] - across[3])
-            flux = (fo[3] + fa[3]) - jnp.maximum(so, sa) * jump
+            flux = 2.0 * (fo[3] + jnp.where(bk, so, -so) * own[3])
             total = total + float(WEIGHTS[i] * WEIGHTS[j]) * flux
     at_wall = (bk & (lane == 127)) | (jnp.logical_not(bk) & (lane == 0))
     loads = jnp.sum(jnp.where(at_wall, total * sign, 0.0), axis=1, keepdims=True)
@@ -220,10 +216,69 @@
 LIFT = COURANT * 0.5 / WEIGHTS[0]
 
 
-def volume_kernel(s_ref, gz_ref, dg_ref, f_ref):
+SCALE = COURANT / SUBSTEPS * 0.5 / WEIGHTS
+
+
+def advance(src, f_ref, sm_ref, gx_ref, gy_ref, gz_ref, put, finish=None):
+    low = jnp.logical_not(row_bit(4))
+    kz = [pair(SCALE[0], SCALE[1]), pair(SCALE[2], SCALE[3])]
+    for c in range(5):
+        done = {}
+        for h in range(2):
+            diff = {}
+            for b in range(4):
+                for d in range(2):
+                    line = [(a, b) if d == 0 else (b, a) for a in range(4)]
+                    g_ref = gx_ref if d == 0 else gy_ref
+                    u = [cell(src, c, *n, h) for n in line]
+                    f = [flux_of(src, f_ref, d, c, *n, h) for n in line]
+                    g = []
+                    for a in range(3):
+                        s = sm_ref[pl.ds(nod(d, *line[a], h), 8), :]
+                        g.append(twice_face(f[a], f[a + 1], s, u[a], u[a + 1]))
+                    if g_ref is None:
+                        diff[d, line[0]], diff[d, line[3]] = g[0], -g[2]
+                    else:
+                        diff[d, line[0]] = g[0] - face_at(g_ref, 0, c, b, h)
+                        diff[d, line[3]] = face_at(g_ref, 1, c, b, h) - g[2]
+                    diff[d, line[1]], diff[d, line[2]] = g[1] - g[0], g[2] - g[1]
+            for i, j in IJ:
+                if SCALE[i] == SCALE[j]:
+                    r = float(SCALE[i]) * (diff[0, (i, j)] + diff[1, (i, j)])
+                else:
+                    r = float(SCALE[i]) * diff[0, (i, j)] + float(SCALE[j]) * diff[1, (i, j)]
+                u = cell(src, c, i, j, h)
+                um = cell(src, c, i, j, 0, 4)
+                fz = flux_of(src, f_ref, 2, c, i, j, h)
+                fm = flux_of(src, f_ref, 2, c, i, j, 0, 4)
+                s = sm_ref[pl.ds(nod(2, i, j, h), 8), :]
+                gz = z_face_at(gz_ref, c, i, j)
+                if h == 0:
+                    t = twice_face(fz, fm, s, u, um)
+                    dz = t - jnp.where(low, gz, turn(t, 4))
+                else:
+                    t = twice_face(fm, fz, s, um, u)
+                    dz = jnp.where(low, turn(t, 4), gz) - t
+                done[i, j, h] = u - (r + kz[h] * dz)
+        for (i, j, h), value in done.items():
+            put(c, i, j, h, value)
+        if finish is not None:
+            finish(c)
+
+
+def outer_faces(value, factor, gx_ref, gy_ref, c, i, j, h):
+    for n, b, g_ref in ((i, j, gx_ref), (j, i, gy_ref)):
+        if n == 0:
+            value = value + float(factor) * face_at(g_ref, 0, c, b, h)
+        if n == 3:
+            value = value - float(factor) * face_at(g_ref, 1, c, b, h)
+    return value
+
+
+def volume_kernel(s_ref, gz_ref, dg_ref, u_ref, f_ref, s3_ref, sm_ref):
     bk = row_bit(4)
     lane = lax.broadcasted_iota(jnp.int32, (8, 128), 1)
-    nodal(s_ref, f_ref)
+    nodal(s_ref, f_ref, s3_ref, sm_ref)
     for i, j in IJ:
         own = [jnp.where(bk, cell(s_ref, c, i, j, 1), cell(s_ref, c, i, j, 0)) for c in range(5)]
         across = z_wall_pair(own, lane)
@@ -262,17 +317,20 @@
                 r = r + (acc[i, j][0] + acc[i, j][1])
                 dg_ref[pl.ds(blk(c, i, j, h), 8), :] = cell(s_ref, c, i, j, h) - r
 
+    def put(c, i, j, h, value):
+        u_ref[pl.ds(blk(c, i, j, h), 8), :] = value
+
+    advance(s_ref, f_ref, sm_ref, None, None, gz_ref, put)
+
 
 def section_kernel(
-    s_ref, slots_ref, ye_ref, yo_ref, xe_ref, xo_ref, gz_ref, dg_ref, result_ref,
+    s_ref, slots_ref, ye_ref, yo_ref, xe_ref, xo_ref, gz_ref, dg_ref, first_ref, result_ref,
     u_ref, f_ref, s3_ref, sm_ref, gx_ref, gy_ref, out_ref, slot_ref, sems,
 ):
     fetch_slot = pltpu.make_async_copy(slots_ref, slot_ref, sems.at[5])
     fetch_slot.start()
-    bx, by, bk = row_bit(2), row_bit(1), row_bit(4)
-    low = jnp.logical_not(bk)
+    bx, by = row_bit(2), row_bit(1)
     ex, ey = parity("group"), parity("dev")
-    nodal(s_ref, f_ref, s3_ref, sm_ref)
     for b in range(4):
         for h in range(2):
             for d, g_ref, even_ref, odd_ref, even, bit, step in (
@@ -294,89 +352,48 @@
                 after = [jnp.where(bit, hh[c], turn(uf[c], -step)) for c in range(5)]
                 fb, sb = point_flux(before, d)
                 fa, sa = point_flux(after, d)
-                sl = jnp.maximum(sb, s3_ref[pl.ds(nod(d, *first, h), 8), :])
-                sh = jnp.maximum(sa, s3_ref[pl.ds(nod(d, *last, h), 8), :])
+                ff, sf = point_flux(uf, d)
+                fl, sl = point_flux(ul, d)
                 for c in range(5):
                     at = ((c * 4 + b) * 2 + h) * 8
                     g_ref[pl.ds(at, 8), :] = twice_face(
-                        fb[c], flux_of(s_ref, f_ref, d, c, *first, h), sl, before[c], uf[c]
+                        fb[c], ff[c], jnp.maximum(sb, sf), before[c], uf[c]
                     )
                     g_ref[pl.ds(320 + at, 8), :] = twice_face(
-                        flux_of(s_ref, f_ref, d, c, *last, h), fa[c], sh, ul[c], after[c]
+                        fl[c], fa[c], jnp.maximum(sa, sl), ul[c], after[c]
                     )
-
-    scale = COURANT / SUBSTEPS * 0.5 / WEIGHTS
-    kz = [pair(scale[0], scale[1]), pair(scale[2], scale[3])]
-
-    def advance(src, put, finish):
-        for c in range(5):
-            done = {}
-            for h in range(2):
-                diff = {}
-                for b in range(4):
-                    for d in range(2):
-                        line = [(a, b) if d == 0 else (b, a) for a in range(4)]
-                        g_ref = gx_ref if d == 0 else gy_ref
-                        u = [cell(src, c, *n, h) for n in line]
-                        f = [flux_of(src, f_ref, d, c, *n, h) for n in line]
-                        g = [face_at(g_ref, 0, c, b, h)]
-                        for a in range(3):
-                            s = sm_ref[pl.ds(nod(d, *line[a], h), 8), :]
-                            g.append(twice_face(f[a], f[a + 1], s, u[a], u[a + 1]))
-                        g.append(face_at(g_ref, 1, c, b, h))
-                        for a in range(4):
-                            diff[d, line[a]] = g[a + 1] - g[a]
-                for i, j in IJ:
-                    if scale[i] == scale[j]:
-                        r = float(scale[i]) * (diff[0, (i, j)] + diff[1, (i, j)])
-                    else:
-                        r = float(scale[i]) * diff[0, (i, j)] + float(scale[j]) * diff[1, (i, j)]
-                    u = cell(src, c, i, j, h)
-                    um = cell(src, c, i, j, 0, 4)
-                    fz = flux_of(src, f_ref, 2, c, i, j, h)
-                    fm = flux_of(src, f_ref, 2, c, i, j, 0, 4)
-                    s = sm_ref[pl.ds(nod(2, i, j, h), 8), :]
-                    gz = z_face_at(gz_ref, c, i, j)
-                    if h == 0:
-                        t = twice_face(fz, fm, s, u, um)
-                        dz = t - jnp.where(low, gz, turn(t, 4))
-                    else:
-                        t = twice_face(fm, fz, s, um, u)
-                        dz = jnp.where(low, turn(t, 4), gz) - t
-                    done[i, j, h] = u - (r + kz[h] * dz)
-            for (i, j, h), value in done.items():
-                put(c, i, j, h, value)
-            finish(c)
 
     def put_u(c, i, j, h, value):
         u_ref[pl.ds(blk(c, i, j, h), 8), :] = value
 
     def put_out(c, i, j, h, value):
         at = pl.ds(blk(c, i, j, h), 8)
-        dg = dg_ref[at, :]
-        for n, b, g_ref in ((i, j, gx_ref), (j, i, gy_ref)):
-            if n == 0:
-                dg = dg + float(LIFT) * face_at(g_ref, 0, c, b, h)
-            if n == 3:
-                dg = dg - float(LIFT) * face_at(g_ref, 1, c, b, h)
+        dg = outer_faces(dg_ref[at, :], LIFT, gx_ref, gy_ref, c, i, j, h)
         out_ref[at, :] = jnp.where(troubled, value, dg)
 
     def store(c):
         rows = pl.ds(c * 256, 256)
         return pltpu.make_async_copy(out_ref.at[rows, :], result_ref.at[rows, :], sems.at[c])
 
-    u_ref[...] = s_ref[...]
+    for c in range(5):
+        for i, j in IJ:
+            for h in range(2):
+                value = first_ref[pl.ds(blk(c, i, j, h), 8), :]
+                put_u(c, i, j, h, outer_faces(value, SCALE[0], gx_ref, gy_ref, c, i, j, h))
+    nodal(u_ref, f_ref, s3_ref, sm_ref)
 
     def substep(_, carry):
-        advance(u_ref, put_u, lambda c: None)
+        advance(u_ref, f_ref, sm_ref, gx_ref, gy_ref, gz_ref, put_u)
         nodal(u_ref, f_ref, s3_ref, sm_ref)
         return carry
 
-    lax.fori_loop(0, SUBSTEPS - 1, substep, 0)
+    lax.fori_loop(0, SUBSTEPS - 2, substep, 0)
     fetch_slot.wait()
     slot = slot_ref[...]
     troubled = jnp.concatenate([slot, slot], axis=0) >= 0
-    advance(u_ref, put_out, lambda c: store(c).start())
+    advance(
+        u_ref, f_ref, sm_ref, gx_ref, gy_ref, gz_ref, put_out, lambda c: store(c).start()
+    )
     for c in range(5):
         store(c).wait()
 
@@ -429,10 +446,18 @@
     small = pltpu.CompilerParams(vmem_limit_bytes=VMEM_LIMIT)
     volume = pl.pallas_call(
         volume_kernel,
-        out_shape=(jax.ShapeDtypeStruct((640, 128), F32), jax.ShapeDtypeStruct((ROWS, 128), F32)),
+        out_shape=(
+            jax.ShapeDtypeStruct((640, 128), F32),
+            jax.ShapeDtypeStruct((ROWS, 128), F32),
+            jax.ShapeDtypeStruct((ROWS, 128), F32),
+        ),
         in_specs=[vmem],
-        out_specs=(vmem, vmem),
-        scratch_shapes=[pltpu.VMEM((9 * 256, 128), F32)],
+        out_specs=(vmem,) * 3,
+        scratch_shapes=[
+            pltpu.VMEM((9 * 256, 128), F32),
+            pltpu.VMEM((3 * 256, 128), F32),
+            pltpu.VMEM((3 * 256, 128), F32),
+        ],
         compiler_params=small,
         name="volume",
         interpret=interpret,
@@ -440,7 +465,7 @@
     section = pl.pallas_call(
         section_kernel,
         out_shape=jax.ShapeDtypeStruct((ROWS, 128), F32),
-        in_specs=[vmem, hbm] + [vmem] * 6,
+        in_specs=[vmem, hbm] + [vmem] * 7,
         out_specs=hbm,
         scratch_shapes=[
             pltpu.VMEM((ROWS, 128), F32),
@@ -458,9 +483,9 @@
         name="section",
         interpret=interpret,
     )
-    gz, dg = volume(rows)
+    gz, dg, first = volume(rows)
     slots = pltpu.with_memory_space_constraint(limit_slot.reshape(4, 128), pltpu.HBM)
-    out = section(rows, slots, ye, yo, xe, xo, gz, dg)
+    out = section(rows, slots, ye, yo, xe, xo, gz, dg, first)
     return out.reshape(state.shape), wall_loads
 
 

time: 41 us -> 40.4 us (0.985)
  waiting for transfers between devices: 11.7 us -> 11 us
    all_to_all x1, waiting for transfers between devices: 11.7 us -> 11 us  [on_device(): parts = lax.all_to_all(part, ('group', 'dev'), 0, 0, tiled=True)]
  transfers between devices with their start and end apart: 5 -> 5, of which waited for: 1 -> 1; matrix products, arithmetic and copies ran while one was open for 0% -> 0% of each run, Pallas kernels for 4% -> 5%
where the time goes in v4:
time: 40.4 us; the launch traced here: 40.3 us
  starting transfers between devices  18.7 us (46%)
  waiting for transfers between devices  11 us (27%)
  Pallas kernels  9.87 us (24%)
  between operations  0.68 us (2%)
    ppermute x4, starting transfers between devices, swap(): return lax.ppermute(x, axis, edges + [(b, a) for a, b in edges])  11.7 us
    all_to_all x1, waiting for transfers between devices, on_device(): parts = lax.all_to_all(part, ('group', 'dev'), 0, 0, tiled=True)  11 us
    all_to_all x1, starting transfers between devices, on_device(): parts = lax.all_to_all(part, ('group', 'dev'), 0, 0, tiled=True)  7 us
    pallas_call x1, Pallas kernels, on_device(): out = section(rows, slots, ye, yo, xe, xo, gz, dg, first)  5.76 us
    pallas_call x1, Pallas kernels, on_device(): pl.pallas_call(prepare_kernel, out_shape=(halo, halo, halo, halo, jax.Sha...  2.02 us
    pallas_call x1, Pallas kernels, on_device(): gz, dg, first = volume(rows)  1.54 us
  transfers between devices with their start and end apart: 5, of which 1 were waited for; matrix products, arithmetic and copies ran while one was open for 0% of the time, Pallas kernels for 5%

profile of v4, /device:TPU:1, one launch (start us, length us, event | category | flops | bytes accessed | tf_op | source)
XLA Modules:
  0.0 40.3 jit_solution(13160185048888086841)
XLA Ops:
  0.6 0.0 copy-start
  0.6 2.0 %prepare.1 = (f32[160,128]{1,0:T(8,128)S(1)}, f32[160,128]{1,0:T(8,128)S(1)}, f32[160,128]{1,0:T(8,128)S(1)}, f32[160,128]{1,0:T(8,128)S(1)}, f32[256,8]{1,0:T(8,128)}) custom-call(f32[1280,128]{1,0:T(8,128)} %bitcast.8, s32[2,2,2]{2,1,0:T(2,128)} %owner_ref.1), custom_call_target="tpu_custom_call" | custom-call | tf_op jit(solution)/shard_map/prepare/pallas_call | solution.py:408
  2.7 2.2 %collective-permute-start = (f32[160,128]{1,0:T(8,128)S(1)}, f32[160,128]{1,0:T(8,128)S(1)}, u32[]{:S(2)}, u32[]{:S(2)}) collective-permute-start(f32[160,128]{1,0:T(8,128)S(1)} %get-tuple-element.10), channel_id=1, source_target_pairs={{0,1},{2,3},{4,5},{6,7},{8,9},{10,11},{12,13},{14,15},{16,17},{18,... | collective-permute-start | bytes 245768 | tf_op jit(solution)/shard_map/ppermute | solution.py:430
  4.9 7.2 %collective-permute-start.1 = (f32[160,128]{1,0:T(8,128)S(1)}, f32[160,128]{1,0:T(8,128)S(1)}, u32[]{:S(2)}, u32[]{:S(2)}) collective-permute-start(f32[160,128]{1,0:T(8,128)S(1)} %get-tuple-element.11), channel_id=1, source_target_pairs={{1,2},{3,4},{5,6},{7,8},{9,10},{11,12},{13,14},{15,16},{17,18},{19... | collective-permute-start | bytes 245768 | tf_op jit(solution)/shard_map/ppermute | solution.py:430
  12.1 1.2 %collective-permute-start.2 = (f32[160,128]{1,0:T(8,128)S(1)}, f32[160,128]{1,0:T(8,128)S(1)}, u32[]{:S(2)}, u32[]{:S(2)}) collective-permute-start(f32[160,128]{1,0:T(8,128)S(1)} %get-tuple-element.12), channel_id=1, source_target_pairs={{0,32},{64,96},{128,160},{192,224},{32,0},{96,64},{160,128},{224,1... | collective-permute-start | bytes 245768 | tf_op jit(solution)/shard_map/ppermute | solution.py:430
  13.3 1.1 %collective-permute-start.3 = (f32[160,128]{1,0:T(8,128)S(1)}, f32[160,128]{1,0:T(8,128)S(1)}, u32[]{:S(2)}, u32[]{:S(2)}) collective-permute-start(f32[160,128]{1,0:T(8,128)S(1)} %get-tuple-element.13), channel_id=1, source_target_pairs={{32,64},{96,128},{160,192},{224,0},{64,32},{128,96},{192,160},{0,2... | collective-permute-start | bytes 245768 | tf_op jit(solution)/shard_map/ppermute | solution.py:430
  14.4 7.0 %all-to-all-start = ((f32[256,1,8]{2,1,0:T(1,128)}), f32[256,1,8]{2,1,0:T(1,128)S(1)}, u32[]{:S(2)}, u32[]{:S(2)}) async-start(f32[256,1,8]{2,1,0:T(1,128)} %bitcast.4), calls=%async_computation | async-start | bytes 262144 | tf_op jit(solution)/shard_map/all_to_all | solution.py:436
  21.4 0.0 copy-done
  21.4 1.5 %volume.1 = (f32[640,128]{1,0:T(8,128)S(1)}, f32[1280,128]{1,0:T(8,128)S(1)}, f32[1280,128]{1,0:T(8,128)S(1)}) custom-call(f32[1280,128]{1,0:T(8,128)S(1)} %bitcast.9), custom_call_target="tpu_custom_call" | custom-call | tf_op jit(solution)/shard_map/volume/pallas_call | solution.py:486
  23.0 11.0 %all-to-all-done = f32[256,1,8]{2,1,0:T(1,128)S(1)} async-done(((f32[256,1,8]{2,1,0:T(1,128)}), f32[256,1,8]{2,1,0:T(1,128)S(1)}, u32[]{:S(2)}, u32[]{:S(2)}) %all-to-all-start) | async-done | bytes 8224 | tf_op jit(solution)/shard_map/all_to_all | solution.py:436
  34.0 0.6 %wall_sum.1 = f32[1,8]{1,0:T(1,128)} custom-call(f32[256,8]{1,0:T(8,128)S(1)} %bitcast.11), custom_call_target="tpu_custom_call" | custom-call | tf_op jit(solution)/shard_map/wall_sum/pallas_call | solution.py:437
  34.5 0.0 collective-permute-done.ye_ref
  34.5 0.0 collective-permute-done.1.yo_ref
  34.5 0.0 collective-permute-done.2.xe_ref
  34.5 0.0 collective-permute-done.3.xo_ref
  34.5 5.8 %section.1 = f32[1280,128]{1,0:T(8,128)} custom-call(f32[1280,128]{1,0:T(8,128)S(1)} %bitcast.10, s32[4,128]{1,0:T(4,128)} %bitcast.13, f32[160,128]{1,0:T(8,128)S(1)} %collective-permute-done.ye_ref, f32[160,128]{1,0:T(8,128)S(1)} %collective-permute-done.1.yo_ref, f32[160,128]{1,0:T(8,128)S(1)} %collective-permute-done.2.xe_ref, ...), custom_call_target="tpu_custom_call" | custom-call | flops 60000000 | bytes 2000000 | tf_op jit(solution)/shard_map/section/pallas_call | solution.py:488
Async XLA Ops:
  0.6 20.8 %copy-start = (f32[5,4,4,4,2,2,128]{6,5,4,3,2,1,0:T(2,128)S(1)}, f32[5,4,4,4,2,2,128]{6,5,4,3,2,1,0:T(2,128)}, u32[]{:S(2)}) copy-start(f32[5,4,4,4,2,2,128]{6,5,4,3,2,1,0:T(2,128)} %param.3) | copy-start | bytes 1966084
  2.7 31.8 %collective-permute-start = (f32[160,128]{1,0:T(8,128)S(1)}, f32[160,128]{1,0:T(8,128)S(1)}, u32[]{:S(2)}, u32[]{:S(2)}) collective-permute-start(f32[160,128]{1,0:T(8,128)S(1)} %get-tuple-element.10), channel_id=1, source_target_pairs={{0,1},{2,3},{4,5},{6,7},{8,9},{10,11},{12,13},{14,15},{16,17},{18,... | collective-permute-start | bytes 245768 | tf_op jit(solution)/shard_map/ppermute | solution.py:430
  4.9 29.7 %collective-permute-start.1 = (f32[160,128]{1,0:T(8,128)S(1)}, f32[160,128]{1,0:T(8,128)S(1)}, u32[]{:S(2)}, u32[]{:S(2)}) collective-permute-start(f32[160,128]{1,0:T(8,128)S(1)} %get-tuple-element.11), channel_id=1, source_target_pairs={{1,2},{3,4},{5,6},{7,8},{9,10},{11,12},{13,14},{15,16},{17,18},{19... | collective-permute-start | bytes 245768 | tf_op jit(solution)/shard_map/ppermute | solution.py:430
  12.1 22.5 %collective-permute-start.2 = (f32[160,128]{1,0:T(8,128)S(1)}, f32[160,128]{1,0:T(8,128)S(1)}, u32[]{:S(2)}, u32[]{:S(2)}) collective-permute-start(f32[160,128]{1,0:T(8,128)S(1)} %get-tuple-element.12), channel_id=1, source_target_pairs={{0,32},{64,96},{128,160},{192,224},{32,0},{96,64},{160,128},{224,1... | collective-permute-start | bytes 245768 | tf_op jit(solution)/shard_map/ppermute | solution.py:430
  13.3 21.2 %collective-permute-start.3 = (f32[160,128]{1,0:T(8,128)S(1)}, f32[160,128]{1,0:T(8,128)S(1)}, u32[]{:S(2)}, u32[]{:S(2)}) collective-permute-start(f32[160,128]{1,0:T(8,128)S(1)} %get-tuple-element.13), channel_id=1, source_target_pairs={{32,64},{96,128},{160,192},{224,0},{64,32},{128,96},{192,160},{0,2... | collective-permute-start | bytes 245768 | tf_op jit(solution)/shard_map/ppermute | solution.py:430
  14.4 19.6 %all-to-all-start = ((f32[256,1,8]{2,1,0:T(1,128)}), f32[256,1,8]{2,1,0:T(1,128)S(1)}, u32[]{:S(2)}, u32[]{:S(2)}) async-start(f32[256,1,8]{2,1,0:T(1,128)} %bitcast.4), calls=%async_computation | async-start | bytes 262144 | tf_op jit(solution)/shard_map/all_to_all | solution.py:436

commit v5 on v4

--- a/solution.py
+++ b/solution.py
@@ -96,16 +96,21 @@
 def prepare_kernel(
     state_ref, owner_ref, ye_ref, yo_ref, xe_ref, xo_ref, part_out_ref, s_ref, own_ref, part_ref, sems
 ):
-    fetch = pltpu.make_async_copy(state_ref, s_ref, sems.at[0])
-    fetch_own = pltpu.make_async_copy(owner_ref, own_ref, sems.at[1])
-    store_part = pltpu.make_async_copy(part_ref, part_out_ref, sems.at[2])
-    fetch.start()
+    def fetch(c):
+        rows = pl.ds(c * 256, 256)
+        return pltpu.make_async_copy(state_ref.at[rows, :], s_ref.at[rows, :], sems.at[c])
+
+    fetch_own = pltpu.make_async_copy(owner_ref, own_ref, sems.at[5])
+    store_part = pltpu.make_async_copy(part_ref, part_out_ref, sems.at[6])
+    for c in range(5):
+        fetch(c).start()
     fetch_own.start()
     part_ref[...] = jnp.zeros(part_ref.shape, F32)
     bx, by, bk = row_bit(2), row_bit(1), row_bit(4)
     lane = lax.broadcasted_iota(jnp.int32, (8, 128), 1)
     ex, ey = parity("group"), parity("dev")
-    fetch.wait()
+    for c in range(5):
+        fetch(c).wait()
     fetch_own.wait()
 
     def get(v, i, j, h):
@@ -414,7 +419,7 @@
             pltpu.VMEM((ROWS, 128), F32),
             pltpu.SMEM((2, 2, 2), jnp.int32),
             pltpu.VMEM((devices, SN_DEV), F32),
-            pltpu.SemaphoreType.DMA((3,)),
+            pltpu.SemaphoreType.DMA((7,)),
         ],
         compiler_params=pltpu.CompilerParams(vmem_limit_bytes=VMEM_LIMIT),
         name="prepare",

time: 40.4 us -> 40.5 us (level)
  no operation moved by 1% of the time
where the time goes in v5:
time: 40.5 us; the launch traced here: 40.4 us
  starting transfers between devices  18.7 us (46%)
  waiting for transfers between devices  11 us (27%)
  Pallas kernels  9.98 us (25%)
  between operations  0.68 us (2%)
    ppermute x4, starting transfers between devices, swap(): return lax.ppermute(x, axis, edges + [(b, a) for a, b in edges])  11.7 us
    all_to_all x1, waiting for transfers between devices, on_device(): parts = lax.all_to_all(part, ('group', 'dev'), 0, 0, tiled=True)  11 us
    all_to_all x1, starting transfers between devices, on_device(): parts = lax.all_to_all(part, ('group', 'dev'), 0, 0, tiled=True)  7 us
    pallas_call x1, Pallas kernels, on_device(): out = section(rows, slots, ye, yo, xe, xo, gz, dg, first)  5.76 us
    pallas_call x1, Pallas kernels, on_device(): pl.pallas_call(prepare_kernel, out_shape=(halo, halo, halo, halo, jax.Sha...  2.12 us
    pallas_call x1, Pallas kernels, on_device(): gz, dg, first = volume(rows)  1.54 us
  transfers between devices with their start and end apart: 5, of which 1 were waited for; matrix products, arithmetic and copies ran while one was open for 0% of the time, Pallas kernels for 5%

profile of v5, /device:TPU:1, one launch (start us, length us, event | category | flops | bytes accessed | tf_op | source)
XLA Modules:
  0.0 40.4 jit_solution(16900195595805390345)
XLA Ops:
  0.6 0.0 copy-start
  0.6 2.1 %prepare.1 = (f32[160,128]{1,0:T(8,128)S(1)}, f32[160,128]{1,0:T(8,128)S(1)}, f32[160,128]{1,0:T(8,128)S(1)}, f32[160,128]{1,0:T(8,128)S(1)}, f32[256,8]{1,0:T(8,128)}) custom-call(f32[1280,128]{1,0:T(8,128)} %bitcast.8, s32[2,2,2]{2,1,0:T(2,128)} %owner_ref.1), custom_call_target="tpu_custom_call" | custom-call | tf_op jit(solution)/shard_map/prepare/pallas_call | solution.py:413
  2.8 2.2 %collective-permute-start = (f32[160,128]{1,0:T(8,128)S(1)}, f32[160,128]{1,0:T(8,128)S(1)}, u32[]{:S(2)}, u32[]{:S(2)}) collective-permute-start(f32[160,128]{1,0:T(8,128)S(1)} %get-tuple-element.10), channel_id=1, source_target_pairs={{0,1},{2,3},{4,5},{6,7},{8,9},{10,11},{12,13},{14,15},{16,17},{18,... | collective-permute-start | bytes 245768 | tf_op jit(solution)/shard_map/ppermute | solution.py:435
  5.0 7.2 %collective-permute-start.1 = (f32[160,128]{1,0:T(8,128)S(1)}, f32[160,128]{1,0:T(8,128)S(1)}, u32[]{:S(2)}, u32[]{:S(2)}) collective-permute-start(f32[160,128]{1,0:T(8,128)S(1)} %get-tuple-element.11), channel_id=1, source_target_pairs={{1,2},{3,4},{5,6},{7,8},{9,10},{11,12},{13,14},{15,16},{17,18},{19... | collective-permute-start | bytes 245768 | tf_op jit(solution)/shard_map/ppermute | solution.py:435
  12.2 1.2 %collective-permute-start.2 = (f32[160,128]{1,0:T(8,128)S(1)}, f32[160,128]{1,0:T(8,128)S(1)}, u32[]{:S(2)}, u32[]{:S(2)}) collective-permute-start(f32[160,128]{1,0:T(8,128)S(1)} %get-tuple-element.12), channel_id=1, source_target_pairs={{0,32},{64,96},{128,160},{192,224},{32,0},{96,64},{160,128},{224,1... | collective-permute-start | bytes 245768 | tf_op jit(solution)/shard_map/ppermute | solution.py:435
  13.4 1.1 %collective-permute-start.3 = (f32[160,128]{1,0:T(8,128)S(1)}, f32[160,128]{1,0:T(8,128)S(1)}, u32[]{:S(2)}, u32[]{:S(2)}) collective-permute-start(f32[160,128]{1,0:T(8,128)S(1)} %get-tuple-element.13), channel_id=1, source_target_pairs={{32,64},{96,128},{160,192},{224,0},{64,32},{128,96},{192,160},{0,2... | collective-permute-start | bytes 245768 | tf_op jit(solution)/shard_map/ppermute | solution.py:435
  14.5 7.0 %all-to-all-start = ((f32[256,1,8]{2,1,0:T(1,128)}), f32[256,1,8]{2,1,0:T(1,128)S(1)}, u32[]{:S(2)}, u32[]{:S(2)}) async-start(f32[256,1,8]{2,1,0:T(1,128)} %bitcast.4), calls=%async_computation | async-start | bytes 262144 | tf_op jit(solution)/shard_map/all_to_all | solution.py:441
  21.5 0.0 copy-done
  21.5 1.5 %volume.1 = (f32[640,128]{1,0:T(8,128)S(1)}, f32[1280,128]{1,0:T(8,128)S(1)}, f32[1280,128]{1,0:T(8,128)S(1)}) custom-call(f32[1280,128]{1,0:T(8,128)S(1)} %bitcast.9), custom_call_target="tpu_custom_call" | custom-call | tf_op jit(solution)/shard_map/volume/pallas_call | solution.py:491
  23.1 11.0 %all-to-all-done = f32[256,1,8]{2,1,0:T(1,128)S(1)} async-done(((f32[256,1,8]{2,1,0:T(1,128)}), f32[256,1,8]{2,1,0:T(1,128)S(1)}, u32[]{:S(2)}, u32[]{:S(2)}) %all-to-all-start) | async-done | bytes 8224 | tf_op jit(solution)/shard_map/all_to_all | solution.py:441
  34.1 0.6 %wall_sum.1 = f32[1,8]{1,0:T(1,128)} custom-call(f32[256,8]{1,0:T(8,128)S(1)} %bitcast.11), custom_call_target="tpu_custom_call" | custom-call | tf_op jit(solution)/shard_map/wall_sum/pallas_call | solution.py:442
  34.6 0.0 collective-permute-done.ye_ref
  34.6 0.0 collective-permute-done.1.yo_ref
  34.6 0.0 collective-permute-done.2.xe_ref
  34.6 0.0 collective-permute-done.3.xo_ref
  34.6 5.8 %section.1 = f32[1280,128]{1,0:T(8,128)} custom-call(f32[1280,128]{1,0:T(8,128)S(1)} %bitcast.10, s32[4,128]{1,0:T(4,128)} %bitcast.13, f32[160,128]{1,0:T(8,128)S(1)} %collective-permute-done.ye_ref, f32[160,128]{1,0:T(8,128)S(1)} %collective-permute-done.1.yo_ref, f32[160,128]{1,0:T(8,128)S(1)} %collective-permute-done.2.xe_ref, ...), custom_call_target="tpu_custom_call" | custom-call | flops 60000000 | bytes 2000000 | tf_op jit(solution)/shard_map/section/pallas_call | solution.py:493
Async XLA Ops:
  0.6 20.9 %copy-start = (f32[5,4,4,4,2,2,128]{6,5,4,3,2,1,0:T(2,128)S(1)}, f32[5,4,4,4,2,2,128]{6,5,4,3,2,1,0:T(2,128)}, u32[]{:S(2)}) copy-start(f32[5,4,4,4,2,2,128]{6,5,4,3,2,1,0:T(2,128)} %param.3) | copy-start | bytes 1966084
  2.8 31.8 %collective-permute-start = (f32[160,128]{1,0:T(8,128)S(1)}, f32[160,128]{1,0:T(8,128)S(1)}, u32[]{:S(2)}, u32[]{:S(2)}) collective-permute-start(f32[160,128]{1,0:T(8,128)S(1)} %get-tuple-element.10), channel_id=1, source_target_pairs={{0,1},{2,3},{4,5},{6,7},{8,9},{10,11},{12,13},{14,15},{16,17},{18,... | collective-permute-start | bytes 245768 | tf_op jit(solution)/shard_map/ppermute | solution.py:435
  5.0 29.7 %collective-permute-start.1 = (f32[160,128]{1,0:T(8,128)S(1)}, f32[160,128]{1,0:T(8,128)S(1)}, u32[]{:S(2)}, u32[]{:S(2)}) collective-permute-start(f32[160,128]{1,0:T(8,128)S(1)} %get-tuple-element.11), channel_id=1, source_target_pairs={{1,2},{3,4},{5,6},{7,8},{9,10},{11,12},{13,14},{15,16},{17,18},{19... | collective-permute-start | bytes 245768 | tf_op jit(solution)/shard_map/ppermute | solution.py:435
  12.2 22.5 %collective-permute-start.2 = (f32[160,128]{1,0:T(8,128)S(1)}, f32[160,128]{1,0:T(8,128)S(1)}, u32[]{:S(2)}, u32[]{:S(2)}) collective-permute-start(f32[160,128]{1,0:T(8,128)S(1)} %get-tuple-element.12), channel_id=1, source_target_pairs={{0,32},{64,96},{128,160},{192,224},{32,0},{96,64},{160,128},{224,1... | collective-permute-start | bytes 245768 | tf_op jit(solution)/shard_map/ppermute | solution.py:435
  13.4 21.2 %collective-permute-start.3 = (f32[160,128]{1,0:T(8,128)S(1)}, f32[160,128]{1,0:T(8,128)S(1)}, u32[]{:S(2)}, u32[]{:S(2)}) collective-permute-start(f32[160,128]{1,0:T(8,128)S(1)} %get-tuple-element.13), channel_id=1, source_target_pairs={{32,64},{96,128},{160,192},{224,0},{64,32},{128,96},{192,160},{0,2... | collective-permute-start | bytes 245768 | tf_op jit(solution)/shard_map/ppermute | solution.py:435
  14.5 19.6 %all-to-all-start = ((f32[256,1,8]{2,1,0:T(1,128)}), f32[256,1,8]{2,1,0:T(1,128)S(1)}, u32[]{:S(2)}, u32[]{:S(2)}) async-start(f32[256,1,8]{2,1,0:T(1,128)} %bitcast.4), calls=%async_computation | async-start | bytes 262144 | tf_op jit(solution)/shard_map/all_to_all | solution.py:441
